TPU v7x, 512 devices: a whole 4x8x8 slice. The times are simulated.
512 devices in a mesh: lat: 64 (over y, z), ma: 8 (over x, core).
Axes of the slice: x: 4, y: 8, z: 8, core: 2. Of those that a mesh axis runs over, the one named last changes fastest.
Arguments:
- pair_wave: int32 [360], replicated, may hold values from 0 to 359, each once
- legendre: bfloat16 [360, 640, 768], P('ma', 'lat'), may hold values from -0.0078125 to 0.0078125
- coefs: bfloat16 [360, 768, 168], P('ma', 'lat'), may hold values from -6 to 6
Outputs:
- noise: float32 [53760, 1440], P(('lat', 'ma'))
Inputs may be any that keep to these rules, and one draw needn't show every extreme that they name: Slot q holds wavenumbers pair_wave[q] and 719 - pair_wave[q]; every value appears once.
All inputs are finite; a program needn't handle non-finite values.
Results may differ from a plain program's by a relative error of at most 0.0003.
Values may be sent and summed in bfloat16 or wider, within the bound.
A program may use at most 64 MiB of HBM per device.

v0:
```python
import math

import jax
import jax.numpy as jnp
from jax import lax
from jax.sharding import PartitionSpec as P

LON = 1440
SINE = [(-1.0) ** n / math.factorial(2 * n + 1) for n in range(6)]


def split_bf16(x):
    hi = lax.reduce_precision(x, 8, 7)
    return hi.astype(jnp.bfloat16), (x - hi).astype(jnp.bfloat16)


def basis_rows(waves, quarter, lon_count):
    positions = jnp.arange(lon_count, dtype=jnp.int32).astype(jnp.float32)
    order = waves.astype(jnp.float32)
    phase = order[:, None] * positions[None, :] + quarter.astype(jnp.float32)[:, None]
    turns = jnp.round(phase * (1.0 / lon_count))
    angle = (phase - turns * lon_count) * (math.pi / lon_count)
    square = angle * angle
    poly = jnp.float32(SINE[-1])
    for coefficient in SINE[-2::-1]:
        poly = poly * square + coefficient
    sine = angle * poly
    weight = jnp.where(waves == 0, 1.0, 2.0).astype(jnp.float32)[:, None]
    return split_bf16(weight - (2.0 * weight) * (sine * sine))


def dot_rows(rows, basis):
    return lax.dot_general(
        rows, basis, (((0,), (0,)), ((), ())), preferred_element_type=jnp.float32
    )


def lay_out(waves, chunks, lat_n):
    parts = []
    start = 0
    for size in chunks:
        stop = start + size * lat_n
        part = waves[:, start : min(stop, waves.shape[1])]
        part = jnp.pad(part, ((0, 0), (0, size * lat_n - part.shape[1])))
        parts.append(part.reshape(-1, lat_n, size))
        start = stop
    return parts


def take_slots(x, axis, start, size):
    stop = min(start + size, x.shape[axis])
    x = lax.slice_in_dim(x, start, stop, axis=axis)
    pads = [(0, 0)] * x.ndim
    pads[axis] = (0, size - (stop - start))
    return jnp.pad(x, pads)


def send_table(legendre, start, size, lat_n):
    rows_dev, _, row_count = legendre.shape
    table = take_slots(legendre, 1, start, size * lat_n)
    table = table.reshape(rows_dev, lat_n, size, row_count).transpose(1, 0, 2, 3)
    return table.reshape(lat_n, rows_dev * size, row_count)


def pack_coefs(coefs, start, size, lat_n, full, group):
    _, deg_dev, cols = coefs.shape
    rest = cols - full
    block = -(-deg_dev // group)
    packed = take_slots(coefs, 0, start, size * lat_n)
    head = packed[..., :full]
    tail = jnp.pad(packed[..., full:], ((0, 0), (0, block * group - deg_dev), (0, 0)))
    tail = jnp.concatenate(
        [tail[:, g * block : (g + 1) * block] for g in range(group)], axis=-1
    )
    tail = jnp.pad(tail, ((0, 0), (0, 0), (0, 128 - group * rest)))
    head = jnp.pad(head, ((0, 0), (0, -deg_dev % 16), (0, 0)))
    both = jnp.concatenate([head, tail], axis=1)
    return both.reshape(lat_n, -1, 128)


def unpack_coefs(both, size, deg_dev, rest, group):
    lat_n = both.shape[0]
    block = -(-deg_dev // group)
    both = both.reshape(lat_n, size, -1, 128)
    head = both[:, :, :deg_dev]
    tail = both[:, :, deg_dev + -deg_dev % 16 :]
    tail = jnp.concatenate(
        [tail[..., g * rest : (g + 1) * rest] for g in range(group)], axis=2
    )
    mine = jnp.concatenate([head, tail[:, :, :deg_dev]], axis=-1)
    return mine.transpose(1, 0, 2, 3).reshape(size, lat_n * deg_dev, -1)


def slot_sums(table, mine, waves, degree_top):
    row_ids = jnp.arange(table.shape[2], dtype=jnp.int32)[None, :]
    split_row = (degree_top - waves)[:, None]
    inside = row_ids < split_row
    outside = (row_ids >= split_row) & (row_ids <= degree_top)
    masks = jnp.stack([inside, outside], axis=1)
    masked = jnp.where(masks[:, :, None, :], table[:, None], jnp.zeros((), table.dtype))
    return jnp.einsum("qhir,qrc->qhic", masked, mine, preferred_element_type=jnp.float32)


def code_rows(sums, lat_n, ma_n):
    size, _, lats, cols = sums.shape
    rows_dev, ch = lats // lat_n, cols // 2
    width = rows_dev * ch // ma_n
    sums = sums.reshape(size, 2, lat_n, rows_dev, 2, ch).transpose(2, 0, 1, 4, 3, 5)
    sums = sums.reshape(lat_n, 2 * size, 2, ma_n, width).transpose(0, 3, 1, 2, 4)
    top = jnp.max(jnp.abs(sums), axis=4, keepdims=True)
    power = jnp.ceil(jnp.log2(jnp.maximum(top, 1e-30)) + 1e-3)
    coded = jnp.round(sums * (jnp.exp2(-power) * 32767.0)).astype(jnp.int16)
    coded = coded.reshape(lat_n * ma_n, 2 * size, 2 * width)
    power = power.astype(jnp.int16).reshape(lat_n * ma_n, 2 * size, 2)
    return jnp.concatenate([coded, power], axis=2)


def decode_rows(coded):
    width = coded.shape[2] // 2 - 1
    scale = jnp.exp2(coded[..., 2 * width :].astype(jnp.float32)) * (1.0 / 32767.0)
    part = jnp.stack([coded[..., :width], coded[..., width : 2 * width]])
    part = part.astype(jnp.float32) * jnp.moveaxis(scale, -1, 0)[..., None]
    hi, lo = split_bf16(part.reshape(-1, width))
    return jnp.concatenate([hi, hi, lo])


def exchange(x, axes):
    return lax.all_to_all(x, axes, split_axis=0, concat_axis=0, tiled=True)


def all_bases(parts, degree_top):
    orders = []
    quarters = []
    for part in parts:
        order = part.transpose(1, 0, 2).reshape(-1, 1)
        order = jnp.concatenate([order, degree_top - 1 - order], axis=1).reshape(-1)
        for e in range(2):
            orders.append(order)
            quarters.append(jnp.full_like(order, e * (LON // 4)))
    hi, lo = basis_rows(jnp.concatenate(orders), jnp.concatenate(quarters), LON)
    bases = []
    start = 0
    for part in parts:
        stop = start + part.size * 4
        bases.append(jnp.concatenate([hi[start:stop], lo[start:stop], hi[start:stop]]))
        start = stop
    return bases


def body(pair_wave, legendre, coefs):
    lat_n = lax.axis_size("lat")
    ma_n = lax.axis_size("ma")
    lat_i = lax.axis_index("lat")
    ma_i = lax.axis_index("ma")
    slots, rows_dev, row_count = legendre.shape
    deg_dev, cols = coefs.shape[1:]
    degree_top = 2 * pair_wave.shape[0]
    per = -(-slots // lat_n)
    per += -per % 4 if per > 4 else 0
    chunks = [per - 4, 4] if per > 4 else [per]
    full = cols // 128 * 128
    rest = cols - full
    group = min(128 // rest, deg_dev)
    parts = lay_out(pair_wave.reshape(ma_n, slots), chunks, lat_n)
    legendre = jnp.transpose(legendre, (1, 0, 2))

    def make_coded(pair, size, part):
        table, both = pair
        mine = unpack_coefs(both, size, deg_dev, rest, group)
        sums = slot_sums(table, mine, part[ma_i, lat_i], degree_top)
        return code_rows(sums, lat_n, ma_n)

    coded_list = []
    ready = None
    arrived = []
    bases = all_bases(parts, degree_top)
    tables = []
    packs = []
    start = 0
    for size in chunks:
        tables.append(send_table(legendre, start, size, lat_n))
        packs.append(pack_coefs(coefs, start, size, lat_n, full, group))
        start += size * lat_n
    table = exchange(jnp.concatenate(tables, axis=1), "lat")
    table, packs, bases = lax.optimization_barrier((table, packs, bases))
    offset = 0
    for k, size in enumerate(chunks):
        both = packs[k]
        if k > 0:
            both, ready = lax.optimization_barrier((both, ready))
        both = exchange(both, "lat")
        ready = both
        if k > 0:
            prev = make_coded(arrived[-1], chunks[k - 1], parts[k - 1])
            both, prev = lax.optimization_barrier((both, prev))
            coded_list.append(prev)
        piece = table[:, offset : offset + rows_dev * size]
        piece = piece.reshape(lat_n * rows_dev, size, row_count).transpose(1, 0, 2)
        both, piece = lax.optimization_barrier((both, piece))
        arrived.append((piece, both))
        offset += rows_dev * size

    if len(chunks) == 1:
        last = make_coded(arrived[-1], chunks[-1], parts[-1])
    total = None
    for k, basis in enumerate(bases):
        coded = exchange(coded_list[k] if k < len(coded_list) else last, ("lat", "ma"))
        if k == len(bases) - 2:
            last = make_coded(arrived[-1], chunks[-1], parts[-1])
            coded, last = lax.optimization_barrier((coded, last))
        term = dot_rows(decode_rows(coded), basis)
        total = term if total is None else total + term
    return total


def solution(mesh):
    in_specs = (P(), P("ma", "lat", None), P("ma", "lat", None))
    out_specs = P(("lat", "ma"), None)
    return jax.shard_map(body, mesh=mesh, in_specs=in_specs, out_specs=out_specs, check_vma=False)
```

profile of v0, /device:TPU:1, one launch (start us, length us, event | category | flops | bytes accessed | tf_op | source)
XLA Modules:
  0.0 138.9 jit_solution(5021695481882190187)
XLA Ops:
  0.0 1.4 copy.87
  1.4 1.3 pad_bitcast_fusion
  2.7 17.1 %all-to-all-start = ((bf16[64,10,768]{2,1,0:T(8,128)(2,1)}), bf16[64,10,768]{2,1,0:T(8,128)(2,1)S(1)}, u32[]{:S(2)}, u32[]{:S(2)}) async-start(bf16[64,10,768]{2,1,0:T(8,128)(2,1)} %pad_bitcast_fusion), calls=%async_computation | async-start | bytes 3145728 | tf_op jit(solution)/shard_map/all_to_all | solution.py:128
  19.8 0.8 reshape.188
  21.2 1.1 copy.67
  22.5 0.8 fusion.24
  23.4 11.2 %fusion = (bf16[2048,1440]{0,1:T(8,128)(2,1)S(1)}, bf16[2048,1440]{0,1:T(8,128)(2,1)S(1)}) fusion(f32[2048]{0:T(1024)} %constant.14.clone.1, f32[1440]{0:T(1024)S(1)} %iota_convert_fusion, f32[2048]{0:T(1024)S(1)} %convert_element_type.53, f32[2048]{0:T(1024)S(1)} %get-tuple-element.30, f32[2048]{0:T(1024)S(1)} %get-tuple-element.29), kind=kLoop, calls=%fused_computation.3 | loop fusion | flops 76677120 | bytes 11835008 | tf_op jit(solution)/shard_map/convert_element_type | solution.py:14
  34.5 7.5 %pad_maximum_fusion = bf16[6144,1440]{0,1:T(8,128)(2,1)} fusion(bf16[2048,1440]{0,1:T(8,128)(2,1)S(1)} %get-tuple-element.26, bf16[2048,1440]{0,1:T(8,128)(2,1)S(1)} %get-tuple-element.25), kind=kLoop, calls=%fused_computation | loop fusion | flops 53084160 | bytes 29491200 | tf_op jit(solution)/shard_map/concatenate | solution.py:145
  42.0 15.4 %all-to-all-done = bf16[64,10,768]{2,1,0:T(8,128)(2,1)S(1)} async-done(((bf16[64,10,768]{2,1,0:T(8,128)(2,1)}), bf16[64,10,768]{2,1,0:T(8,128)(2,1)S(1)}, u32[]{:S(2)}, u32[]{:S(2)}) %all-to-all-start) | async-done | bytes 983072 | tf_op jit(solution)/shard_map/all_to_all | solution.py:128
  57.4 10.4 %all-to-all-start.1 = ((bf16[64,20,128]{2,1,0:T(8,128)(2,1)}), bf16[64,20,128]{2,1,0:T(8,128)(2,1)S(1)}, u32[]{:S(2)}, u32[]{:S(2)}) async-start(bf16[64,20,128]{2,1,0:T(8,128)(2,1)} %fusion.24), calls=%async_computation.1 | async-start | bytes 786432 | tf_op jit(solution)/shard_map/all_to_all | solution.py:128
  67.8 0.7 fusion.35
  68.5 0.6 compare_and_fusion
  69.6 11.9 %all-to-all-done.1 = bf16[64,20,128]{2,1,0:T(8,128)(2,1)S(1)} async-done(((bf16[64,20,128]{2,1,0:T(8,128)(2,1)}), bf16[64,20,128]{2,1,0:T(8,128)(2,1)S(1)}, u32[]{:S(2)}, u32[]{:S(2)}) %all-to-all-start.1) | async-done | bytes 327712 | tf_op jit(solution)/shard_map/all_to_all | solution.py:128
  82.9 0.7 fusion.14
  83.6 0.8 copy.72
  84.5 0.8 reshape.195
  85.3 0.5 fusion.18
  86.3 0.4 copy.75
  87.6 0.5 copy.78
  88.1 36.0 %all_to_all.15 = s16[512,2,212]{2,1,0:T(2,128)(2,1)S(1)} all-to-all(s16[512,2,212]{2,1,0:T(2,128)(2,1)S(1)} %copy.78), channel_id=1, replica_groups=mesh['lat'=64,'ma'=8] {'lat','ma'}, dimensions={0} | all-to-all | bytes 868352 | tf_op jit(solution)/shard_map/all_to_all | solution.py:128
  124.1 0.6 slice.58
  125.5 0.7 slice_bitcast_fusion.1
  126.2 0.6 pad_add_fusion.1
  127.1 11.8 %fusion.8 = f32[105,1440]{1,0:T(8,128)} fusion(bf16[6144,1440]{0,1:T(8,128)(2,1)} %pad_maximum_fusion, bf16[2048,105]{1,0:T(8,128)(2,1)S(1)} %get-tuple-element.16, bf16[2048,105]{1,0:T(8,128)(2,1)S(1)} %get-tuple-element.15), kind=kOutput, calls=%fused_computation.15 | convolution fusion | flops 1861816320 | bytes 19159680 | tf_op jit(solution)/shard_map/dot_general | solution.py:33
  (37 shorter events, 5.2 us)
Async XLA Ops:
  2.7 54.8 %all-to-all-start = ((bf16[64,10,768]{2,1,0:T(8,128)(2,1)}), bf16[64,10,768]{2,1,0:T(8,128)(2,1)S(1)}, u32[]{:S(2)}, u32[]{:S(2)}) async-start(bf16[64,10,768]{2,1,0:T(8,128)(2,1)} %pad_bitcast_fusion), calls=%async_computation | async-start | bytes 3145728 | tf_op jit(solution)/shard_map/all_to_all | solution.py:128
  57.4 24.0 %all-to-all-start.1 = ((bf16[64,20,128]{2,1,0:T(8,128)(2,1)}), bf16[64,20,128]{2,1,0:T(8,128)(2,1)S(1)}, u32[]{:S(2)}, u32[]{:S(2)}) async-start(bf16[64,20,128]{2,1,0:T(8,128)(2,1)} %fusion.24), calls=%async_computation.1 | async-start | bytes 786432 | tf_op jit(solution)/shard_map/all_to_all | solution.py:128
where the time goes:
time: 139 us
  blocking collectives  36 us (26%)
  starting transfers between devices  27.5 us (20%)
  waiting for transfers between devices  27.3 us (20%)
  other arithmetic  23.3 us (17%)
  matrix products  12.5 us (9%)
  local copies, waits for them, and re-layouts  12.1 us (9%)
    all_to_all x1, blocking collectives, exchange(): return lax.all_to_all(x, axes, split_axis=0, concat_axis=0, tiled=True)  36 us
    all_to_all x2, starting transfers between devices, exchange(): return lax.all_to_all(x, axes, split_axis=0, concat_axis=0, tiled=True)  27.5 us
    all_to_all x2, waiting for transfers between devices, exchange(): return lax.all_to_all(x, axes, split_axis=0, concat_axis=0, tiled=True)  27.3 us
    dot_general x1, matrix products, dot_rows(): lax.dot_general(rows, basis, (((0,), (0,)), ((), ())), preferred_element_...  11.8 us
    convert_element_type x2, other arithmetic, split_bf16(): return (hi.astype(jnp.bfloat16), (x - hi).astype(jnp.bfloat16))  11.5 us
    concatenate x1, other arithmetic, all_bases(): jnp.concatenate([hi[start:stop], lo[start:stop], hi[start:stop]])  7.5 us
  transfers between devices with their start and end apart: 2, of which 2 were waited for; matrix products, arithmetic and copies ran while one was open for 17% of the time, Pallas kernels for 0%

commit v1 on v0

v1 whole, which is shorter than its diff:
```python
import functools
import math

import jax
import jax.numpy as jnp
from jax import lax
from jax.experimental import pallas as pl
from jax.experimental.pallas import tpu as pltpu
from jax.sharding import PartitionSpec as P

LON = 1440
HALF = 720
RING = 8
ORDER = (1, 7, 2, 6, 3, 5, 4)
GROUP = 6
CH = 84
SINE = [(-1.0) ** n / math.factorial(2 * n + 1) for n in range(6)]
MESH = pl.DeviceIdType.MESH


def split_bf16(x):
    hi = lax.reduce_precision(x, 8, 7)
    return hi.astype(jnp.bfloat16), (x - hi).astype(jnp.bfloat16)


def basis_rows(waves, quarter):
    positions = jnp.arange(HALF, dtype=jnp.int32).astype(jnp.float32)
    order = waves.astype(jnp.float32)
    phase = order[:, None] * positions[None, :] + quarter.astype(jnp.float32)[:, None]
    turns = jnp.round(phase * (1.0 / LON))
    angle = (phase - turns * LON) * (math.pi / LON)
    square = angle * angle
    poly = jnp.float32(SINE[-1])
    for coefficient in SINE[-2::-1]:
        poly = poly * square + coefficient
    sine = angle * poly
    weight = jnp.where(waves == 0, 1.0, 2.0).astype(jnp.float32)[:, None]
    return split_bf16(weight - (2.0 * weight) * (sine * sine))


def pack_table(legendre):
    slots, rows_dev, row_count = legendre.shape
    table = jnp.pad(legendre, ((0, RING * GROUP - slots), (0, 0), (0, 0)))
    head = table[:, :8].reshape(RING, 2, 24, row_count)
    tail = table[:, 8:].reshape(RING, 2, 6, row_count)
    tail = jnp.pad(tail, ((0, 0), (0, 0), (0, 2), (0, 0)))
    return jnp.concatenate([head, tail], axis=2)


def pack_coefs(coefs):
    slots, deg_dev, cols = coefs.shape
    x = jnp.pad(coefs, ((0, RING * GROUP - slots), (0, 0), (0, 0)))
    x = x.reshape(RING, 2, 3, deg_dev, 2, CH).transpose(0, 1, 4, 3, 2, 5)
    x = x.reshape(RING, 2, 2, deg_dev, 3 * CH)
    x = jnp.pad(x, ((0, 0),) * 4 + ((0, 256 - 3 * CH),))
    x = x.reshape(RING, 2, 2, deg_dev, 2, 128).transpose(0, 1, 2, 4, 3, 5)
    return x.reshape(RING, 8 * deg_dev, 128)


def sums_kernel(
    waves, table, packs, out,
    table_in, packs_in, wide, coef_rows, coef_all, coded, back,
    c_send, c_recv, l_send, l_recv, r_send, r_recv,
    b_send, b_recv, m_send, m_recv, local,
):
    lat = lax.axis_index("lat")
    ma = lax.axis_index("ma")
    y = lat // RING
    z = lax.rem(lat, RING)
    z_to = [lax.rem(z + d, RING) for d in ORDER]
    z_from = [lax.rem(z + RING - d, RING) for d in ORDER]
    ma_to = [lax.rem(ma + d, RING) for d in ORDER]
    up = (lax.rem(y + 1, RING) * RING + z, ma)
    down = (lax.rem(y + RING - 1, RING) * RING + z, ma)

    barrier = pltpu.get_barrier_semaphore()
    targets = [(y * RING + p, ma) for p in z_to] + [(lat, p) for p in ma_to] + [up, down]
    for target in targets:
        pl.semaphore_signal(barrier, inc=1, device_id=target, device_id_type=MESH)
    pl.semaphore_wait(barrier, len(targets))

    def remote(src, dst, send, recv, target):
        copy = pltpu.make_async_remote_copy(
            src_ref=src, dst_ref=dst, send_sem=send, recv_sem=recv,
            device_id=target, device_id_type=MESH,
        )
        copy.start()
        return copy

    c_copies = [
        remote(packs.at[p], packs_in.at[z], c_send.at[k], c_recv.at[k], (y * RING + p, ma))
        for k, p in enumerate(z_to)
    ]
    own_c = pltpu.make_async_copy(packs.at[z], packs_in.at[z], local.at[0])
    own_c.start()
    own_l = pltpu.make_async_copy(table.at[z], table_in.at[z], local.at[1])
    own_l.start()
    l_copies = []
    for a in range(2):
        for k, p in enumerate(z_to):
            l_copies.append(
                remote(table.at[p, a], table_in.at[z, a], l_send.at[a, k], l_recv.at[a, k], (y * RING + p, ma))
            )

    own_c.wait()
    for copy in c_copies:
        copy.wait_recv()
    deg_dev = packs.shape[1] // 8
    for s in range(RING):
        wide[s] = packs_in[s].astype(jnp.float32)
    for a in range(2):
        for s in range(RING):
            for t in range(4):
                piece = wide[s, pl.ds((a * 4 + t) * deg_dev, deg_dev), :]
                coef_rows[a, pl.ds(s * deg_dev, deg_dev), pl.ds(t * 128, 128)] = piece
        coef_all[y, a] = coef_rows[a].astype(jnp.bfloat16)

    piece_rows = coef_all.shape[2] // 2

    def ring_send(dirn, step, s):
        org = lax.rem(y + (RING - step if dirn == 0 else step), RING)
        ref = coef_all.at[org, s // 2, pl.ds((s % 2) * piece_rows, piece_rows)]
        return remote(ref, ref, r_send.at[dirn, step, s], r_recv.at[dirn, step, s], up if dirn == 0 else down)

    def hops(dirn, s):
        return 4 if (s % 2 == 0) == (dirn == 0) else 3

    live = {}
    for s in range(4):
        for dirn in range(2):
            live[dirn, 0, s] = ring_send(dirn, 0, s)
    for step in range(1, 5):
        for s in range(4):
            for dirn in range(2):
                if step <= hops(dirn, s):
                    live[dirn, step - 1, s].wait_recv()
                    if step < hops(dirn, s):
                        live[dirn, step, s] = ring_send(dirn, step, s)

    own_l.wait()
    for copy in l_copies:
        copy.wait_recv()

    row = lax.broadcasted_iota(jnp.int32, (32, 1), 0)
    member = jnp.where(row < 24, row // 8, (row - 24) // 2)
    column = lax.broadcasted_iota(jnp.int32, (1, 1, table.shape[3]), 2)
    lane = lax.rem(lax.broadcasted_iota(jnp.int32, (1, 1, 512), 2), 256)
    lane_out = lax.broadcasted_iota(jnp.int32, (1, 1, 128), 2)
    last = waves.shape[0] // RING - 1
    for a in range(2):
        bounds = []
        for b in range(3):
            slot = jnp.minimum(z * GROUP + a * 3 + b, last)
            u = waves[ma * (last + 1) + slot]
            cut = HALF - u
            even = (u & 1) == 0
            bounds.append((
                (jnp.where(even, 0, cut), jnp.where(even, cut, HALF + 1)),
                (jnp.where(even, cut, 0), jnp.where(even, HALF + 1, cut)),
            ))
        rows_a = table_in[:, a].astype(jnp.float32)
        rhs = coef_all[:, a].reshape(-1, 512)
        for par in range(2):
            low, high = [
                jnp.where(member == 0, bounds[0][par][j], jnp.where(member == 1, bounds[1][par][j], bounds[2][par][j]))[None]
                for j in range(2)
            ]
            keep = (column >= low) & (column < high)
            lhs = jnp.where(keep, rows_a, 0.0).astype(jnp.bfloat16).reshape(256, -1)
            sums = jnp.dot(lhs, rhs, preferred_element_type=jnp.float32)
            sums = sums.reshape(RING, 4, 8, 512)
            tail = sums[:, 3]
            two, four = pltpu.roll(tail, 6, 1), pltpu.roll(tail, 4, 1)
            parts = (
                (0, 8, (sums[:, 0], sums[:, 1], sums[:, 2])),
                (8, 2, (tail, two, four)),
            )
            for start, count, (s0, s1, s2) in parts:
                value = jnp.where(lane < CH, s0, jnp.where(lane < 2 * CH, s1, s2))
                value = jnp.where(lane < 3 * CH, value, 0.0)
                top = jnp.max(jnp.abs(value), axis=2, keepdims=True)
                power = jnp.ceil(jnp.log2(jnp.maximum(top, 1e-30)) + 1e-3)
                code = jnp.round(value * (jnp.exp2(-power) * 32767.0)).astype(jnp.int32)
                word = (code[:, :, :256] << 16) | (code[:, :, 256:] & 0xFFFF)
                first, second = word[:, :, :128], word[:, :, 128:]
                second = jnp.where(lane_out == 3 * CH - 128, power.astype(jnp.int32), second)
                for half, item in enumerate((first, second)):
                    coded[:, start : start + count, a * 4 + par * 2 + half, :] = item[:, :count]

    b_copies = [
        remote(coded.at[p], back.at[z], b_send.at[k], b_recv.at[k], (y * RING + p, ma))
        for k, p in enumerate(z_to)
    ]
    m_copies = []
    own = []

    def forward(k, src, zs):
        for j, p in enumerate(ma_to):
            m_copies.append(
                remote(src.at[pl.ds((5 * p) // 4, 2)], out.at[ma, zs], m_send.at[k, j], m_recv.at[k, j], (lat, p))
            )
        copy = pltpu.make_async_copy(src.at[pl.ds((5 * ma) // 4, 2)], out.at[ma, zs], local.at[2 + k])
        copy.start()
        own.append(copy)

    forward(7, coded.at[z], z)
    for k, zs in enumerate(z_from):
        b_copies[k].wait_recv()
        forward(k, back.at[zs], zs)
    for copy in c_copies + l_copies + list(live.values()) + b_copies:
        copy.wait_send()
    for copy in own:
        copy.wait()
    for copy in m_copies:
        copy.wait()


def sums_call(waves, table, packs):
    vmem = pl.BlockSpec(memory_space=pltpu.VMEM)
    dma = pltpu.SemaphoreType.DMA
    deg = packs.shape[1] // 8 * RING
    return pl.pallas_call(
        sums_kernel,
        out_shape=jax.ShapeDtypeStruct((RING, RING, 2, 8, 128), jnp.int32),
        in_specs=[pl.BlockSpec(memory_space=pltpu.SMEM), vmem, vmem],
        out_specs=vmem,
        scratch_shapes=[
            pltpu.VMEM(table.shape, jnp.bfloat16),
            pltpu.VMEM(packs.shape, jnp.bfloat16),
            pltpu.VMEM(packs.shape, jnp.float32),
            pltpu.VMEM((2, deg, 512), jnp.float32),
            pltpu.VMEM((RING, 2, deg, 512), jnp.bfloat16),
            pltpu.VMEM((RING, 10, 8, 128), jnp.int32),
            pltpu.VMEM((RING, 10, 8, 128), jnp.int32),
            dma((7,)), dma((7,)), dma((2, 7)), dma((2, 7)),
            dma((2, 4, 4)), dma((2, 4, 4)),
            dma((7,)), dma((7,)), dma((8, 7)), dma((8, 7)), dma((10,)),
        ],
        compiler_params=pltpu.CompilerParams(
            collective_id=0, has_side_effects=True, vmem_limit_bytes=40 << 20
        ),
        name="sums",
    )(waves, table, packs)


def body(pair_wave, legendre, coefs):
    ma_i = lax.axis_index("ma")
    slots = legendre.shape[0]
    table, packs = pack_table(legendre), pack_coefs(coefs)
    local = jnp.minimum(jnp.arange(RING * GROUP), slots - 1)
    waves = pair_wave.reshape(RING, slots)[:, local]
    even = jnp.where(waves % 2 == 0, waves, HALF - 1 - waves).reshape(-1)
    orders = jnp.stack([even, even, HALF - 1 - even, HALF - 1 - even])
    quarters = jnp.broadcast_to(jnp.array([[0], [LON // 4]] * 2), orders.shape)
    hi, lo = basis_rows(orders.reshape(-1), quarters.reshape(-1))
    hi, lo = hi.reshape(2, -1, HALF), lo.reshape(2, -1, HALF)
    basis = jnp.concatenate([hi, lo, hi], axis=1)

    words = sums_call(pair_wave, table, packs)
    words = words.reshape(RING, RING, 2, 2, 2, 256)
    power = words[..., 3 * CH : 3 * CH + 1]
    scale = jnp.exp2(power.astype(jnp.float32)) * (1.0 / 32767.0)
    words = words[..., : 3 * CH]
    both = jnp.stack([words >> 16, (words << 16) >> 16])
    value = both.astype(jnp.float32) * scale[None]
    value = value.reshape(2, RING, RING, 2, 2, 2, 3, CH)
    value = value.transpose(5, 0, 1, 2, 4, 6, 3, 7).reshape(2, -1, 2 * CH)
    hi, lo = split_bf16(value)
    rows = jnp.concatenate([hi, hi, lo], axis=1)
    both = lax.dot_general(
        rows, basis, (((1,), (1,)), ((0,), (0,))), preferred_element_type=jnp.float32
    )
    start = 105 * ma_i - CH * ((5 * ma_i) // 4)
    both = lax.dynamic_slice_in_dim(both, start, 105, axis=1)
    return jnp.concatenate([both[0] + both[1], both[0] - both[1]], axis=1)


def solution(mesh):
    in_specs = (P(), P("ma", "lat", None), P("ma", "lat", None))
    out_specs = P(("lat", "ma"), None)
    return jax.shard_map(body, mesh=mesh, in_specs=in_specs, out_specs=out_specs, check_vma=False)
```

time: 139 us -> 76.3 us (0.55)
  Pallas kernels: 0 us -> 56.7 us
  blocking collectives: 36 us -> 0 us
  starting transfers between devices: 27.5 us -> 0 us
  waiting for transfers between devices: 27.3 us -> 0 us
  other arithmetic: 23.3 us -> 6.47 us
  matrix products: 12.5 us -> 2.41 us
  local copies, waits for them, and re-layouts: 12.1 us -> 10.3 us
    pallas_call x0 -> x1, Pallas kernels: none -> 56.7 us  [sums_call(): pl.pallas_call(sums_kernel, out_shape=jax.ShapeDtypeStruct((RING, RING, 2...]
    all_to_all x1 -> x0, blocking collectives: 36 us -> none  [exchange(): return lax.all_to_all(x, axes, split_axis=0, concat_axis=0, tiled=True)]
    all_to_all x2 -> x0, starting transfers between devices: 27.5 us -> none  [exchange(): return lax.all_to_all(x, axes, split_axis=0, concat_axis=0, tiled=True)]
    all_to_all x2 -> x0, waiting for transfers between devices: 27.3 us -> none  [exchange(): return lax.all_to_all(x, axes, split_axis=0, concat_axis=0, tiled=True)]
    dot_general x2 -> x1, matrix products: 12.5 us -> 2.41 us  [body(): lax.dot_general(rows, basis, (((1,), (1,)), ((0,), (0,))), preferred_elem...]
    concatenate x6 -> x2, other arithmetic: 8.99 us -> 1.1 us  [the longest x1 1.03 us: body(): return jnp.concatenate([both[0] + both[1], both[0] - both[1]], axis=1)]
    convert_element_type x2, other arithmetic: 11.5 us -> 4.17 us  [split_bf16(): return (hi.astype(jnp.bfloat16), (x - hi).astype(jnp.bfloat16))]
    reshape x5 -> x10, local copies, waits for them, and re-layouts: 3.27 us -> 3.11 us  [the longest x2 1.34 us: body(): value = value.transpose(5, 0, 1, 2, 4, 6, 3, 7).reshape(2, -1, 2 * CH)]
  transfers between devices with their start and end apart: 2 -> 0, of which waited for: 2 -> 0; matrix products, arithmetic and copies ran while one was open for 17% -> 0% of each run, Pallas kernels for 0% -> 0%
where the time goes in v1:
time: 76.3 us; the launch traced here: 76.1 us
  Pallas kernels  56.7 us (74%)
  local copies, waits for them, and re-layouts  10.3 us (13%)
  other arithmetic  6.47 us (8%)
  matrix products  2.41 us (3%)
    pallas_call x1, Pallas kernels, sums_call(): pl.pallas_call(sums_kernel, out_shape=jax.ShapeDtypeStruct((RING, RING, 2...  56.7 us
    convert_element_type x2, other arithmetic, split_bf16(): return (hi.astype(jnp.bfloat16), (x - hi).astype(jnp.bfloat16))  4.17 us
    dot_general x1, matrix products, body(): lax.dot_general(rows, basis, (((1,), (1,)), ((0,), (0,))), preferred_elem...  2.41 us
    unnamed x7, local copies, waits for them, and re-layouts  1.55 us

profile of v1, /device:TPU:1, one launch (start us, length us, event | category | flops | bytes accessed | tf_op | source)
XLA Modules:
  0.0 76.1 jit_solution(18024599035603892241)
XLA Ops:
  0.0 0.8 reshape.234
  0.8 0.8 broadcast_bitcast_fusion
  1.6 0.6 gather_fusion
  2.5 0.9 %pad_slice_fusion = bf16[48,2,768]{2,0,1:T(8,128)(2,1)S(1)} fusion(bf16[45,10,768]{2,0,1:T(8,128)(2,1)} %param.5), kind=kLoop, calls=%fused_computation.32 | loop fusion | bytes 838656 | tf_op jit(solution)/shard_map/slice | solution.py:45
  3.6 1.1 %pad.18 = bf16[48,12,168]{2,0,1:T(8,128)(2,1)S(1)} pad(bf16[45,12,168]{2,0,1:T(8,128)(2,1)} %param.6, bf16[]{:T(256)} %constant.27.clone.1), padding=0_3x0_0x0_0 | pad | bytes 374978 | tf_op jit(solution)/shard_map/jit(_pad)/pad | solution.py:52
  4.7 0.2 reshape.228
  5.0 0.2 reshape.229
  5.4 0.2 copy.10
  5.6 0.3 copy-done
  6.0 56.7 %sums.1 = s32[8,8,2,8,128]{4,3,2,1,0:T(8,128)S(1)} custom-call(s32[360]{0:T(512)S(1)} %copy-done, bf16[8,2,32,768]{3,2,1,0:T(8,128)(2,1)S(1)} %fusion.19.table, bf16[8,96,128]{2,1,0:T(8,128)(2,1)S(1)} %copy.14.packs), custom_call_target="tpu_custom_call" | custom-call | tf_op jit(solution)/shard_map/sums/pallas_call | solution.py:222
  62.6 0.3 reshape.232
  63.0 0.3 slice.29
  63.3 0.5 copy.24
  63.8 0.2 copy_shift-right-arithmetic_fusion
  64.0 0.4 stack.14
  64.5 0.4 stack.15
  64.9 0.8 %fusion.11 = f32[2,2,8,8,2,3,2,84]{7,5,3,0,4,6,2,1:T(4,128)S(1)} fusion(s32[1,8,8,2,2,2,3,84]{7,6,2,5,4,3,1,0:T(4,128)S(1)} %stack.15, s32[1,8,8,2,2,2,3,84]{7,6,2,5,4,3,1,0:T(4,128)S(1)} %stack.14, f32[8,8,2,2,2]{1,4,3,2,0:T(2,128)S(1)} %copy.17), kind=kLoop, calls=%fused_computation.19 | loop fusion | flops 774144 | bytes 2066432 | tf_op jit(solution)/shard_map/transpose | solution.py:267
  65.7 1.2 %copy.18 = f32[2,2,8,8,2,3,2,84]{7,6,5,4,3,2,1,0:T(2,128)S(1)} copy(f32[2,2,8,8,2,3,2,84]{7,5,3,0,4,6,2,1:T(4,128)S(1)} %fusion.11) | data formatting | bytes 2064384 | tf_op jit(solution)/shard_map/transpose | solution.py:267
  67.0 0.9 %reshape.233 = f32[2,768,168]{2,1,0:T(8,128)S(1)} reshape(f32[2,2,8,8,2,3,2,84]{7,6,5,4,3,2,1,0:T(2,128)S(1)} %copy.18) | data formatting | bytes 2064384 | tf_op jit(solution)/shard_map/reshape | solution.py:267
  67.9 0.4 copy.19
  68.3 0.1 reduce-precision_convert_fusion.1
  68.5 4.0 %fusion.6 = (bf16[2,768,720]{1,2,0:T(8,128)(2,1)S(1)}, bf16[2,768,720]{1,2,0:T(8,128)(2,1)S(1)}) fusion(f32[2,768]{1,0:T(2,128)S(1)} %bitcast.43, f32[720]{0:T(1024)S(1)} %iota_convert_fusion, f32[2,768]{1,0:T(2,128)S(1)} %convert_element_type.65, f32[2,768]{1,0:T(2,128)S(1)} %broadcast_multiply_fusion, f32[2,768]{1,0:T(2,128)S(1)} %select_n.60), kind=kLoop, calls=%fused_computation.9 | loop fusion | flops 28753920 | bytes 4451136 | tf_op jit(solution)/shard_map/convert_element_type | solution.py:23
  72.5 2.4 %fusion = f32[2,168,720]{2,1,0:T(8,128)S(1)} fusion(bf16[2,768,720]{1,2,0:T(8,128)(2,1)S(1)} %get-tuple-element.14, bf16[2,768,720]{1,2,0:T(8,128)(2,1)S(1)} %get-tuple-element.13, bf16[2,768,168]{1,2,0:T(8,128)(2,1)S(1)} %get-tuple-element.10, bf16[2,768,168]{1,2,0:T(8,128)(2,1)S(1)} %get-tuple-element.9), kind=kOutput, calls=%fused_computation.1 | convolution fusion | flops 1139318784 | bytes 6423552 | tf_op jit(solution)/shard_map/dot_general | solution.py:270
  75.0 1.0 %pad_maximum_fusion = f32[105,1440]{1,0:T(8,128)} fusion(f32[105,720]{1,0:T(8,128)S(1)} %get-tuple-element.8, f32[105,720]{1,0:T(8,128)S(1)} %get-tuple-element.7), kind=kLoop, calls=%fused_computation.31 | loop fusion | flops 151200 | bytes 1209600 | tf_op jit(solution)/shard_map/concatenate | solution.py:275
  (27 shorter events, 1.0 us)
Async XLA Ops:
  3.4 1.9 %copy-start.1 = (bf16[45,10,768]{2,0,1:T(8,128)(2,1)S(1)}, bf16[45,10,768]{2,0,1:T(8,128)(2,1)}, u32[]{:S(2)}) copy-start(bf16[45,10,768]{2,0,1:T(8,128)(2,1)} %param.5) | copy-start | bytes 2073604
  5.3 0.7 copy-start

commit v2 on v1

v2 whole, which is shorter than its diff:
```python
import math

import jax
import jax.numpy as jnp
from jax import lax
from jax.experimental import pallas as pl
from jax.experimental.pallas import tpu as pltpu
from jax.sharding import PartitionSpec as P

LON = 1440
HALF = 720
RING = 8
ORDER = (1, 7, 2, 6, 3, 5, 4)
TABLE_STEPS = ((4, 5), (2, 3), (6,), (0, 1))
BASIS_STEPS = (3, 2, 1, 0)
CH = 84
SINE = [(-1.0) ** n / math.factorial(2 * n + 1) for n in range(6)]
COSINE = [(-1.0) ** n / math.factorial(2 * n) for n in range(7)]
MESH = pl.DeviceIdType.MESH


def pack_table(legendre):
    slots, rows_dev, row_count = legendre.shape
    table = jnp.pad(legendre, ((0, 6 * RING - slots), (0, 0), (0, 0)))
    head = table[:, :8].reshape(2, RING, 24, row_count)
    tail = table[:, 8:].reshape(2, RING, 6, row_count)
    tail = jnp.pad(tail, ((0, 0), (0, 0), (0, 2), (0, 0)))
    return jnp.concatenate([head, tail], axis=2)


def pack_coefs(coefs):
    slots, deg_dev, cols = coefs.shape
    x = jnp.pad(coefs, ((0, 6 * RING - slots), (0, 0), (0, 0)))
    x = x.reshape(2, RING, 3, deg_dev, 2, CH).transpose(0, 1, 4, 3, 2, 5)
    x = x.reshape(2, RING, 2, deg_dev, 3 * CH)
    x = jnp.pad(x, ((0, 0),) * 4 + ((0, 256 - 3 * CH),))
    x = x.reshape(2, RING, 2, deg_dev, 2, 128).transpose(0, 1, 2, 4, 3, 5)
    return x.reshape(2, RING, 4 * deg_dev, 128)


def poly(coefficients, square):
    value = jnp.float32(coefficients[-1])
    for coefficient in coefficients[-2::-1]:
        value = value * square + coefficient
    return value


def turn(phase):
    turns = jnp.round(phase * (1.0 / LON))
    angle = (phase - turns * LON) * (math.pi / LON)
    square = angle * angle
    sine = angle * poly(SINE, square)
    return 1.0 - 2.0 * (sine * sine), 2.0 * (sine * poly(COSINE, square))


def split_bf16(x):
    hi = x.astype(jnp.bfloat16)
    return hi, (x - hi.astype(jnp.float32)).astype(jnp.bfloat16)


def synth_kernel(
    waves, table, packs, out,
    table_in, packs_in, wide, coef_rows, coef_all, coded, back, words,
    perm, orders, basis, turned, rows, total,
    c_send, c_recv, l_send, l_recv, r_send, r_recv,
    b_send, b_recv, m_send, m_recv, local,
):
    lat = lax.axis_index("lat")
    ma = lax.axis_index("ma")
    y = lat // RING
    z = lax.rem(lat, RING)
    group = (z, y)
    place = (y, z)
    to = [[lax.rem(group[a] + d, RING) for d in ORDER] for a in range(2)]
    source = [[lax.rem(group[a] + RING - d, RING) for d in ORDER] for a in range(2)]
    ma_to = [lax.rem(ma + d, RING) for d in ORDER]

    def peer(a, p):
        return (y * RING + p, ma) if a == 0 else (p * RING + z, ma)

    next_to = [
        [peer(1 - a, lax.rem(place[a] + step, RING)) for step in (1, RING - 1)]
        for a in range(2)
    ]

    barrier = pltpu.get_barrier_semaphore()
    targets = [peer(a, p) for a in range(2) for p in to[a]] + [(lat, p) for p in ma_to]
    for target in targets:
        pl.semaphore_signal(barrier, inc=1, device_id=target, device_id_type=MESH)
    pl.semaphore_wait(barrier, len(targets))

    def remote(src, dst, send, recv, target):
        copy = pltpu.make_async_remote_copy(
            src_ref=src, dst_ref=dst, send_sem=send, recv_sem=recv,
            device_id=target, device_id_type=MESH,
        )
        copy.start()
        return copy

    def keep_local(src, dst, sem):
        copy = pltpu.make_async_copy(src, dst, sem)
        copy.start()
        return copy

    c_copies = [[], []]
    for k in range(7):
        for a in range(2):
            p = to[a][k]
            c_copies[a].append(
                remote(packs.at[a, p], packs_in.at[a, group[a]], c_send.at[a, k], c_recv.at[a, k], peer(a, p))
            )
    own_c = [keep_local(packs.at[a, group[a]], packs_in.at[a, group[a]], local.at[a]) for a in range(2)]
    own_l = [keep_local(table.at[a, group[a]], table_in.at[a, group[a]], local.at[2 + a]) for a in range(2)]
    l_copies = [[], []]

    def send_table(ks):
        for k in ks:
            for a in range(2):
                p = to[a][k]
                l_copies[a].append(
                    remote(table.at[a, p], table_in.at[a, group[a]], l_send.at[a, k], l_recv.at[a, k], peer(a, p))
                )

    send_table(TABLE_STEPS[0])

    pairs = waves.shape[1]
    per = pairs // RING
    wave_row = waves[...].astype(jnp.float32)

    def waves_of(slot):
        lanes = lax.broadcasted_iota(jnp.int32, (slot.shape[0], pairs), 1)
        return jnp.sum(jnp.where(lanes == slot, wave_row, 0.0), axis=1, keepdims=True)

    row = lax.broadcasted_iota(jnp.int32, (6 * RING * RING, 1), 0)
    block, inner = row // (RING * RING), lax.rem(row, RING * RING)
    part, member = block // 3, lax.rem(block, 3)
    slot = jnp.minimum(part * 3 * RING + lax.rem(inner, RING) * 3 + member, per - 1)
    found = waves_of((inner // RING) * per + slot)
    orders[...] = jnp.broadcast_to(found, orders.shape)

    lane = lax.broadcasted_iota(jnp.int32, (1, 128), 1).astype(jnp.float32)

    def make_basis(block):
        u = orders[pl.ds(pl.multiple_of(block * 64, 64), 64), :]
        half = jnp.floor(u * 0.5) * 2.0
        even = jnp.where(half == u, u, (HALF - 1.0) - u)
        for par in range(2):
            order = even if par == 0 else (HALF - 1.0) - even
            weight = jnp.where(order == 0.0, 1.0, 2.0)
            cos, sin = turn(order * lane)
            cos, sin = weight * cos, weight * sin
            cos_t, sin_t = turn(order * (lane * 128.0))
            for t in range(6):
                ct, st = cos_t[:, t : t + 1], sin_t[:, t : t + 1]
                for e, value in enumerate((cos * ct - sin * st, -(sin * ct + cos * st))):
                    hi, lo = split_bf16(value)
                    for j, item in enumerate((hi, hi, lo)):
                        basis[par, block, pl.ds(j * 128 + e * 64, 64), pl.ds(t * 128, 128)] = item

    def make_bases(start, count):
        lax.fori_loop(start, start + count, lambda n, c: (make_basis(n), c)[1], 0)

    column = lax.broadcasted_iota(jnp.int32, (1, table.shape[3]), 1)
    deg_dev = packs.shape[2] // 4
    deg = RING * deg_dev
    turned_column = (
        lax.rem(column, deg) // deg_dev * deg + column // deg * deg_dev + lax.rem(column, deg_dev)
    )
    natural = lax.broadcasted_iota(jnp.int32, perm.shape, 0)
    perm[...] = jnp.where(natural == turned_column, 1.0, 0.0).astype(jnp.bfloat16)
    made = 0
    make_bases(made, BASIS_STEPS[0])
    made += BASIS_STEPS[0]

    def ring_send(a, dirn, step, s):
        org = lax.rem(place[a] + (RING - step if dirn == 0 else step), RING)
        ref = coef_all.at[a, org, pl.ds(s * (deg // 2), deg // 2)]
        return remote(ref, ref, r_send.at[a, dirn, step, s], r_recv.at[a, dirn, step, s], next_to[a][dirn])

    def hops(dirn, s):
        return 4 if s == dirn else 3

    live = {}
    for a in range(2):
        own_c[a].wait()
        for copy in c_copies[a]:
            copy.wait_recv()
        wide[a] = packs_in[a].astype(jnp.float32)
        for s in range(RING):
            for t in range(4):
                piece = wide[a, s, pl.ds(t * deg_dev, deg_dev), :]
                coef_rows[a, pl.ds(s * deg_dev, deg_dev), pl.ds(t * 128, 128)] = piece
        coef_all[a, place[a]] = coef_rows[a].astype(jnp.bfloat16)
        for s in range(2):
            for dirn in range(2):
                live[a, dirn, 0, s] = ring_send(a, dirn, 0, s)
    for step in range(1, 5):
        if step < 4:
            send_table(TABLE_STEPS[step])
            if BASIS_STEPS[step]:
                make_bases(made, BASIS_STEPS[step])
                made += BASIS_STEPS[step]
        for a in range(2):
            for s in range(2):
                for dirn in range(2):
                    if step <= hops(dirn, s):
                        live[a, dirn, step - 1, s].wait_recv()
                        if step < hops(dirn, s):
                            live[a, dirn, step, s] = ring_send(a, dirn, step, s)

    row = lax.broadcasted_iota(jnp.int32, (32, 1), 0)
    member = jnp.minimum(jnp.where(row < 24, row // 8, (row - 24) // 2), 2)
    lane_in = lax.rem(lax.broadcasted_iota(jnp.int32, (1, 1, 512), 2), 256)
    lane_out = lax.broadcasted_iota(jnp.int32, (1, 1, 128), 2)

    def make_coded(a):
        own_l[a].wait()
        for copy in l_copies[a]:
            copy.wait_recv()
        u = waves_of(ma * per + jnp.minimum(a * 3 * RING + group[a] * 3 + member, per - 1))
        cut = HALF - u
        even = jnp.floor(u * 0.5) * 2.0 == u
        bounds = (
            (jnp.where(even, 0.0, cut), jnp.where(even, cut, HALF + 1.0)),
            (jnp.where(even, cut, 0.0), jnp.where(even, HALF + 1.0, cut)),
        )
        if a == 0:
            rows_a = table_in[0].astype(jnp.float32)
            at = column
        else:
            flat = table_in[1].reshape(RING * 32, -1)
            rows_a = jnp.dot(flat, perm[...], preferred_element_type=jnp.float32).reshape(RING, 32, -1)
            at = turned_column
        at = at.astype(jnp.float32)
        rhs = coef_all[a].reshape(-1, 512)
        for par in range(2):
            low, high = bounds[par]
            keep = ((at >= low) & (at < high))[None]
            lhs = jnp.where(keep, rows_a, 0.0).astype(jnp.bfloat16).reshape(RING * 32, -1)
            sums = jnp.dot(lhs, rhs, preferred_element_type=jnp.float32)
            sums = sums.reshape(RING, 4, 8, 512)
            tail = sums[:, 3]
            two, four = pltpu.roll(tail, 6, 1), pltpu.roll(tail, 4, 1)
            parts = (
                (0, 8, (sums[:, 0], sums[:, 1], sums[:, 2])),
                (8, 2, (tail, two, four)),
            )
            for start, count, (s0, s1, s2) in parts:
                value = jnp.where(lane_in < CH, s0, jnp.where(lane_in < 2 * CH, s1, s2))
                value = jnp.where(lane_in < 3 * CH, value, 0.0)
                top = jnp.max(jnp.abs(value), axis=2, keepdims=True)
                power = jnp.ceil(jnp.log2(jnp.maximum(top, 1e-30)) + 1e-3)
                code = jnp.round(value * (jnp.exp2(-power) * 32767.0)).astype(jnp.int32)
                word = (code[:, :, :256] << 16) | (code[:, :, 256:] & 0xFFFF)
                first, second = word[:, :, :128], word[:, :, 128:]
                second = jnp.where(lane_out == 3 * CH - 128, power.astype(jnp.int32), second)
                for half, item in enumerate((first, second)):
                    coded[a, :, start : start + count, par * 2 + half, :] = item[:, :count]

    b_copies = [[], []]
    m_copies = [[], []]
    own_m = [[], []]

    def forward(a, k, src, sent):
        for j, p in enumerate(ma_to):
            m_copies[a].append(
                remote(
                    src.at[pl.ds((5 * p) // 4, 2)], words.at[a, ma, sent],
                    m_send.at[a, k, j], m_recv.at[a, k, j], (lat, p),
                )
            )
        own_m[a].append(
            keep_local(src.at[pl.ds((5 * ma) // 4, 2)], words.at[a, ma, sent], local.at[4 + 8 * a + k])
        )

    def send_coded(a):
        for k in range(7):
            p = to[a][k]
            b_copies[a].append(
                remote(coded.at[a, p], back.at[a, group[a]], b_send.at[a, k], b_recv.at[a, k], peer(a, p))
            )
        forward(a, 7, coded.at[a, group[a]], group[a])

    def forward_all(a):
        for k in range(7):
            b_copies[a][k].wait_recv()
            forward(a, k, back.at[a, source[a][k]], source[a][k])

    def synthesize(a):
        for copy in own_m[a]:
            copy.wait()
        for copy in m_copies[a]:
            copy.wait_recv()
        for par in range(2):
            for i in range(2):
                first = words[a, :, :, i, par * 2, :].reshape(64, 128)
                second = words[a, :, :, i, par * 2 + 1, :].reshape(64, 128)
                power = second[:, 3 * CH - 128 : 3 * CH - 127].astype(jnp.float32)
                scale = jnp.exp2(power) * (1.0 / 32767.0)
                for half, word in enumerate((first, second)):
                    real = (word >> 16).astype(jnp.float32) * scale
                    imag = ((word << 16) >> 16).astype(jnp.float32) * scale
                    both = jnp.concatenate([real, imag], axis=0)
                    turned[pl.ds(half * 128, 128), :] = both.T
                for b in range(3):
                    hi, lo = split_bf16(turned[pl.ds(b * CH, 96), :])
                    for j, item in enumerate((hi, lo, hi)):
                        rows[par, pl.ds(i * 96, 96), pl.ds((b * 3 + j) * 128, 128)] = item
            term = jnp.dot(
                rows[par], basis[par, 3 * a : 3 * a + 3].reshape(1152, -1), preferred_element_type=jnp.float32
            )
            if a == 0:
                total[par] = term
            else:
                total[par] += term

    turned[pl.ds(256, turned.shape[0] - 256), :] = jnp.zeros((turned.shape[0] - 256, 128), jnp.float32)
    make_coded(0)
    send_coded(0)
    make_coded(1)
    send_coded(1)
    forward_all(0)
    forward_all(1)
    synthesize(0)
    synthesize(1)

    edge = HALF - 640
    lanes = lax.broadcasted_iota(jnp.int32, (1, 128), 1)
    for i in range(2):
        even, odd = total[0, pl.ds(i * 96, CH), :], total[1, pl.ds(i * 96, CH), :]
        plus = even + odd
        minus = pltpu.roll(even - odd, edge, 1)
        at = pl.ds(i * CH, CH)
        out[at, :640] = plus[:, :640]
        out[at, 640:768] = jnp.where(lanes < edge, plus[:, 640:], minus[:, :128])
        out[at, 768:1408] = minus[:, 128:]
        out[at, 1408:] = minus[:, : LON - 1408]

    for a in range(2):
        for copy in c_copies[a] + l_copies[a] + b_copies[a] + m_copies[a]:
            copy.wait_send()
    for copy in live.values():
        copy.wait_send()


def synth_call(waves, table, packs):
    vmem = pl.BlockSpec(memory_space=pltpu.VMEM)
    dma = pltpu.SemaphoreType.DMA
    deg = packs.shape[2] // 4 * RING
    deg_all = table.shape[3]
    f32, bf16, s32 = jnp.float32, jnp.bfloat16, jnp.int32
    return pl.pallas_call(
        synth_kernel,
        out_shape=jax.ShapeDtypeStruct((2 * CH, LON), f32),
        in_specs=[vmem, vmem, vmem],
        out_specs=vmem,
        scratch_shapes=[
            pltpu.VMEM(table.shape, bf16),
            pltpu.VMEM(packs.shape, bf16),
            pltpu.VMEM(packs.shape, f32),
            pltpu.VMEM((2, deg, 512), f32),
            pltpu.VMEM((2, RING, deg, 512), bf16),
            pltpu.VMEM((2, RING, 10, 4, 128), s32),
            pltpu.VMEM((2, RING, 10, 4, 128), s32),
            pltpu.VMEM((2, RING, RING, 2, 4, 128), s32),
            pltpu.VMEM((deg_all, deg_all), bf16),
            pltpu.VMEM((6 * 64, 128), f32),
            pltpu.VMEM((2, 6, 384, 768), bf16),
            pltpu.VMEM((272, 128), f32),
            pltpu.VMEM((2, 192, 1152), bf16),
            pltpu.VMEM((2, 192, 768), f32),
            dma((2, 7)), dma((2, 7)), dma((2, 7)), dma((2, 7)),
            dma((2, 2, 4, 2)), dma((2, 2, 4, 2)),
            dma((2, 7)), dma((2, 7)), dma((2, 8, 7)), dma((2, 8, 7)), dma((20,)),
        ],
        compiler_params=pltpu.CompilerParams(
            collective_id=0, has_side_effects=True, vmem_limit_bytes=48 << 20
        ),
        name="synth",
    )(waves, table, packs)


def body(pair_wave, legendre, coefs):
    ma_i = lax.axis_index("ma")
    table, packs = pack_table(legendre), pack_coefs(coefs)
    both = synth_call(pair_wave.reshape(1, -1), table, packs)
    start = 105 * ma_i - CH * ((5 * ma_i) // 4)
    return lax.dynamic_slice_in_dim(both, start, 105, axis=0)


def solution(mesh):
    in_specs = (P(), P("ma", "lat", None), P("ma", "lat", None))
    out_specs = P(("lat", "ma"), None)
    return jax.shard_map(body, mesh=mesh, in_specs=in_specs, out_specs=out_specs, check_vma=False)
```

time: 76.3 us -> 63.1 us (0.83)
  other arithmetic: 6.47 us -> 0.07 us
  local copies, waits for them, and re-layouts: 10.3 us -> 4.53 us
  matrix products: 2.41 us -> 0 us
  Pallas kernels: 56.7 us -> 58.2 us
    convert_element_type x4 -> x0, other arithmetic: 4.19 us -> none  [the longest x2 4.17 us: split_bf16(): return (hi.astype(jnp.bfloat16), (x - hi).astype(jnp.bfloat16))]
    dot_general x1 -> x0, matrix products: 2.41 us -> none  [body(): lax.dot_general(rows, basis, (((1,), (1,)), ((0,), (0,))), preferred_elem...]
    reshape x10 -> x6, local copies, waits for them, and re-layouts: 3.11 us -> 1.34 us  [the longest x1 0.75 us: body(): both = synth_call(pair_wave.reshape(1, -1), table, packs)]
    pallas_call x1, Pallas kernels: 56.7 us -> 58.2 us  [synth_call(): pl.pallas_call(synth_kernel, out_shape=jax.ShapeDtypeStruct((2 * CH, LON)...]
    transpose x3 -> x2, local copies, waits for them, and re-layouts: 1.32 us -> 0.07 us  [pack_coefs(): x = x.reshape(2, RING, 2, deg_dev, 2, 128).transpose(0, 1, 2, 4, 3, 5)]
    concatenate x1 -> x0, other arithmetic: 1.03 us -> none  [body(): return jnp.concatenate([both[0] + both[1], both[0] - both[1]], axis=1)]
    pad x1, local copies, waits for them, and re-layouts: 1.05 us -> 0.05 us  [pack_coefs(): x = jnp.pad(coefs, ((0, 6 * RING - slots), (0, 0), (0, 0)))]
    dynamic_slice x0 -> x1, local copies, waits for them, and re-layouts: none -> 0.93 us  [body(): return lax.dynamic_slice_in_dim(both, start, 105, axis=0)]
where the time goes in v2:
time: 63.1 us; the launch traced here: 63 us
  Pallas kernels  58.2 us (92%)
  local copies, waits for them, and re-layouts  4.53 us (7%)
    pallas_call x1, Pallas kernels, synth_call(): pl.pallas_call(synth_kernel, out_shape=jax.ShapeDtypeStruct((2 * CH, LON)...  58.2 us

profile of v2, /device:TPU:1, one launch (start us, length us, event | category | flops | bytes accessed | tf_op | source)
XLA Modules:
  0.0 63.0 jit_solution(8600439863165266115)
XLA Ops:
  0.0 0.0 copy-start
  0.0 0.8 %reshape.21.waves = s32[1,360]{1,0:T(1,128)S(1)} reshape(s32[360]{0:T(512)} %param.3) | data formatting | bytes 2880 | tf_op jit(solution)/shard_map/reshape | solution.py:386
  0.8 0.9 %pad_slice_fusion = bf16[48,2,768]{2,0,1:T(8,128)(2,1)S(1)} fusion(bf16[45,10,768]{2,0,1:T(8,128)(2,1)} %param.4), kind=kLoop, calls=%fused_computation.3 | loop fusion | bytes 838656 | tf_op jit(solution)/shard_map/slice | solution.py:26
  1.7 0.1 copy.7
  1.8 0.1 reshape.23
  1.9 0.0 copy-done
  1.9 0.2 copy.6
  2.1 0.0 copy-start.1
  2.1 0.1 fusion.1.table
  2.2 0.9 %copy-done.1 = bf16[45,12,168]{2,0,1:T(8,128)(2,1)S(1)} copy-done((bf16[45,12,168]{2,0,1:T(8,128)(2,1)S(1)}, bf16[45,12,168]{2,0,1:T(8,128)(2,1)}, u32[]{:S(2)}) %copy-start.1) | copy-done | bytes 181464
  3.1 0.1 pad.18
  3.1 0.2 reshape.24
  3.3 0.1 copy.12
  3.5 0.2 reshape.25
  3.8 58.2 %synth.1 = f32[168,1440]{1,0:T(8,128)S(1)} custom-call(s32[1,360]{1,0:T(1,128)S(1)} %reshape.21.waves, bf16[2,8,32,768]{3,2,1,0:T(8,128)(2,1)S(1)} %fusion.1.table, bf16[2,8,48,128]{3,2,1,0:T(8,128)(2,1)S(1)} %copy.10.packs), custom_call_target="tpu_custom_call" | custom-call | tf_op jit(solution)/shard_map/synth/pallas_call | solution.py:352
  62.0 0.9 %constant_dynamic-slice_fusion = f32[105,1440]{1,0:T(8,128)} fusion(f32[168,1440]{1,0:T(8,128)S(1)} %synth.1, s32[]{:T(128)S(6)} %select_n.9), kind=kLoop, calls=%fused_computation.7 | loop fusion | bytes 1209604 | tf_op jit(solution)/shard_map/dynamic_slice | solution.py:388
  (4 shorter events, 0.1 us)
Async XLA Ops:
  0.0 1.9 %copy-start = (bf16[45,10,768]{2,0,1:T(8,128)(2,1)S(1)}, bf16[45,10,768]{2,0,1:T(8,128)(2,1)}, u32[]{:S(2)}) copy-start(bf16[45,10,768]{2,0,1:T(8,128)(2,1)} %param.4) | copy-start | bytes 2073604
  2.1 1.0 %copy-start.1 = (bf16[45,12,168]{2,0,1:T(8,128)(2,1)S(1)}, bf16[45,12,168]{2,0,1:T(8,128)(2,1)}, u32[]{:S(2)}) copy-start(bf16[45,12,168]{2,0,1:T(8,128)(2,1)} %param.5) | copy-start | bytes 544324

commit v3 on v2

--- a/solution.py
+++ b/solution.py
@@ -60,10 +60,10 @@
 
 def synth_kernel(
     waves, table, packs, out,
-    table_in, packs_in, wide, coef_rows, coef_all, coded, back, words,
-    perm, orders, basis, turned, rows, total,
+    table_in, packs_in, wide, coef_rows, coef_all, raw, coded, back, words,
+    perm, orders, basis, turned, blocks, rows, total,
     c_send, c_recv, l_send, l_recv, r_send, r_recv,
-    b_send, b_recv, m_send, m_recv, local,
+    b_send, b_recv, m_send, m_recv, own_sem,
 ):
     lat = lax.axis_index("lat")
     ma = lax.axis_index("ma")
@@ -72,7 +72,6 @@
     group = (z, y)
     place = (y, z)
     to = [[lax.rem(group[a] + d, RING) for d in ORDER] for a in range(2)]
-    source = [[lax.rem(group[a] + RING - d, RING) for d in ORDER] for a in range(2)]
     ma_to = [lax.rem(ma + d, RING) for d in ORDER]
 
     def peer(a, p):
@@ -102,24 +101,21 @@
         copy.start()
         return copy
 
-    c_copies = [[], []]
-    for k in range(7):
+    def wait_bytes(ref, sem):
+        pltpu.make_async_copy(ref, ref, sem).wait()
+
+    for k in range(6, -1, -1):
         for a in range(2):
             p = to[a][k]
-            c_copies[a].append(
-                remote(packs.at[a, p], packs_in.at[a, group[a]], c_send.at[a, k], c_recv.at[a, k], peer(a, p))
-            )
-    own_c = [keep_local(packs.at[a, group[a]], packs_in.at[a, group[a]], local.at[a]) for a in range(2)]
-    own_l = [keep_local(table.at[a, group[a]], table_in.at[a, group[a]], local.at[2 + a]) for a in range(2)]
-    l_copies = [[], []]
+            remote(packs.at[a, p], packs_in.at[a, group[a]], c_send.at[a], c_recv.at[a], peer(a, p))
+    own_c = [keep_local(packs.at[a, group[a]], packs_in.at[a, group[a]], own_sem.at[0, a]) for a in range(2)]
+    own_l = [keep_local(table.at[a, group[a]], table_in.at[a, group[a]], own_sem.at[1, a]) for a in range(2)]
 
     def send_table(ks):
         for k in ks:
             for a in range(2):
                 p = to[a][k]
-                l_copies[a].append(
-                    remote(table.at[a, p], table_in.at[a, group[a]], l_send.at[a, k], l_recv.at[a, k], peer(a, p))
-                )
+                remote(table.at[a, p], table_in.at[a, group[a]], l_send.at[a], l_recv.at[a], peer(a, p))
 
     send_table(TABLE_STEPS[0])
 
@@ -134,7 +130,10 @@
     row = lax.broadcasted_iota(jnp.int32, (6 * RING * RING, 1), 0)
     block, inner = row // (RING * RING), lax.rem(row, RING * RING)
     part, member = block // 3, lax.rem(block, 3)
-    slot = jnp.minimum(part * 3 * RING + lax.rem(inner, RING) * 3 + member, per - 1)
+    near = lax.rem(inner, RING)
+    step = jnp.where(lax.rem(near, 2) == 1, (near + 1) // 2, RING - near // 2)
+    came = lax.rem(jnp.where(part == 0, group[0], group[1]) + RING - step, RING)
+    slot = jnp.minimum(part * 3 * RING + came * 3 + member, per - 1)
     found = waves_of((inner // RING) * per + slot)
     orders[...] = jnp.broadcast_to(found, orders.shape)
 
@@ -175,7 +174,7 @@
     def ring_send(a, dirn, step, s):
         org = lax.rem(place[a] + (RING - step if dirn == 0 else step), RING)
         ref = coef_all.at[a, org, pl.ds(s * (deg // 2), deg // 2)]
-        return remote(ref, ref, r_send.at[a, dirn, step, s], r_recv.at[a, dirn, step, s], next_to[a][dirn])
+        return remote(ref, ref, r_send.at[a], r_recv.at[a, dirn, step, s], next_to[a][dirn])
 
     def hops(dirn, s):
         return 4 if s == dirn else 3
@@ -183,8 +182,7 @@
     live = {}
     for a in range(2):
         own_c[a].wait()
-        for copy in c_copies[a]:
-            copy.wait_recv()
+        wait_bytes(packs_in.at[a, pl.ds(0, 7)], c_recv.at[a])
         wide[a] = packs_in[a].astype(jnp.float32)
         for s in range(RING):
             for t in range(4):
@@ -194,29 +192,33 @@
         for s in range(2):
             for dirn in range(2):
                 live[a, dirn, 0, s] = ring_send(a, dirn, 0, s)
-    for step in range(1, 5):
-        if step < 4:
-            send_table(TABLE_STEPS[step])
-            if BASIS_STEPS[step]:
-                make_bases(made, BASIS_STEPS[step])
-                made += BASIS_STEPS[step]
+
+    def ring_step(a, step):
+        for s in range(2):
+            for dirn in range(2):
+                if step <= hops(dirn, s):
+                    live[a, dirn, step - 1, s].wait_recv()
+                    if step < hops(dirn, s):
+                        live[a, dirn, step, s] = ring_send(a, dirn, step, s)
+
+    for step in range(1, 4):
+        send_table(TABLE_STEPS[step])
+        if BASIS_STEPS[step]:
+            make_bases(made, BASIS_STEPS[step])
+            made += BASIS_STEPS[step]
         for a in range(2):
-            for s in range(2):
-                for dirn in range(2):
-                    if step <= hops(dirn, s):
-                        live[a, dirn, step - 1, s].wait_recv()
-                        if step < hops(dirn, s):
-                            live[a, dirn, step, s] = ring_send(a, dirn, step, s)
+            ring_step(a, step)
 
     row = lax.broadcasted_iota(jnp.int32, (32, 1), 0)
     member = jnp.minimum(jnp.where(row < 24, row // 8, (row - 24) // 2), 2)
     lane_in = lax.rem(lax.broadcasted_iota(jnp.int32, (1, 1, 512), 2), 256)
-    lane_out = lax.broadcasted_iota(jnp.int32, (1, 1, 128), 2)
+    lane_out = lax.broadcasted_iota(jnp.int32, (1, 256), 1)
+    lane_left = lax.broadcasted_iota(jnp.int32, (1, 128), 1)
 
     def make_coded(a):
+        ring_step(a, 4)
         own_l[a].wait()
-        for copy in l_copies[a]:
-            copy.wait_recv()
+        wait_bytes(table_in.at[a, pl.ds(0, 7)], l_recv.at[a])
         u = waves_of(ma * per + jnp.minimum(a * 3 * RING + group[a] * 3 + member, per - 1))
         cut = HALF - u
         even = jnp.floor(u * 0.5) * 2.0 == u
@@ -252,60 +254,81 @@
                 power = jnp.ceil(jnp.log2(jnp.maximum(top, 1e-30)) + 1e-3)
                 code = jnp.round(value * (jnp.exp2(-power) * 32767.0)).astype(jnp.int32)
                 word = (code[:, :, :256] << 16) | (code[:, :, 256:] & 0xFFFF)
-                first, second = word[:, :, :128], word[:, :, 128:]
-                second = jnp.where(lane_out == 3 * CH - 128, power.astype(jnp.int32), second)
-                for half, item in enumerate((first, second)):
-                    coded[a, :, start : start + count, par * 2 + half, :] = item[:, :count]
-
-    b_copies = [[], []]
-    m_copies = [[], []]
-    own_m = [[], []]
-
-    def forward(a, k, src, sent):
-        for j, p in enumerate(ma_to):
-            m_copies[a].append(
-                remote(
-                    src.at[pl.ds((5 * p) // 4, 2)], words.at[a, ma, sent],
-                    m_send.at[a, k, j], m_recv.at[a, k, j], (lat, p),
-                )
-            )
-        own_m[a].append(
-            keep_local(src.at[pl.ds((5 * ma) // 4, 2)], words.at[a, ma, sent], local.at[4 + 8 * a + k])
-        )
+                word = jnp.where(lane_in[:, :, :256] < 3 * CH, word, power.astype(jnp.int32))
+                raw[par, :, start : start + count, :] = word[:, :count]
+        for p in range(RING):
+            i0, cut = (5 * p) // 4, 21 * (p % 4)
+            left = None
+            for par in range(2):
+                one, two = raw[par, :, i0, :], raw[par, :, i0 + 1, :]
+                main = one
+                if cut:
+                    near = pltpu.roll(one, 256 - cut, 1)
+                    main = jnp.where(lax.rem(lane_out, CH) < CH - cut, near, pltpu.roll(two, CH - cut, 1))
+                main = jnp.where(lane_out < 3 * CH, main, jnp.where(lane_out == 3 * CH, one, two))
+                for half in range(2):
+                    coded[a, :, p * 5 + par * 2 + half, 0, :] = main[:, half * 128 : half * 128 + 128]
+                for b in range(3):
+                    shift = 63 * par - 63 * b - cut
+                    item = (pltpu.roll(two, shift % 256, 1) if shift else two)[:, :128]
+                    left = item if left is None else jnp.where(lane_left < 63 * par + 21 * b, left, item)
+            coded[a, :, p * 5 + 4, 0, :] = left
+
+    own_b = []
+    own_m = []
 
     def send_coded(a):
+        own_b.append(keep_local(coded.at[a, group[a]], back.at[a, 0], own_sem.at[2, a]))
         for k in range(7):
             p = to[a][k]
-            b_copies[a].append(
-                remote(coded.at[a, p], back.at[a, group[a]], b_send.at[a, k], b_recv.at[a, k], peer(a, p))
+            remote(coded.at[a, p], back.at[a, k + 1], b_send.at[a], b_recv.at[a, (k + 1) // 4], peer(a, p))
+
+    def forward(a, batch):
+        if batch == 0:
+            own_b[a].wait()
+            wait_bytes(back.at[a, pl.ds(1, 3)], b_recv.at[a, 0])
+        else:
+            wait_bytes(back.at[a, pl.ds(4, 4)], b_recv.at[a, 1])
+        four = pl.ds(4 * batch, 4)
+        for p in ma_to:
+            remote(
+                back.at[a, four, pl.ds(5 * p, 5)], words.at[a, ma, four],
+                m_send.at[a], m_recv.at[a], (lat, p),
             )
-        forward(a, 7, coded.at[a, group[a]], group[a])
-
-    def forward_all(a):
-        for k in range(7):
-            b_copies[a][k].wait_recv()
-            forward(a, k, back.at[a, source[a][k]], source[a][k])
+        own_m.append(keep_local(back.at[a, four, pl.ds(5 * ma, 5)], words.at[a, ma, four], own_sem.at[3 + batch, a]))
+
+    limit = CH - 21 * lax.rem(ma, 4)
+
+    def plane(a, k):
+        return words[a, :, :, k, 0, :].reshape(64, 128)
+
+    def unit(power):
+        return jnp.exp2(power.astype(jnp.float32)) * (1.0 / 32767.0)
+
+    def turned_rows(word, scale):
+        real = (word >> 16).astype(jnp.float32) * scale
+        imag = ((word << 16) >> 16).astype(jnp.float32) * scale
+        return jnp.concatenate([real, imag], axis=0).T
 
     def synthesize(a):
-        for copy in own_m[a]:
-            copy.wait()
-        for copy in m_copies[a]:
-            copy.wait_recv()
+        wait_bytes(words.at[a, pl.ds(0, 7)], m_recv.at[a])
+        scales = []
         for par in range(2):
-            for i in range(2):
-                first = words[a, :, :, i, par * 2, :].reshape(64, 128)
-                second = words[a, :, :, i, par * 2 + 1, :].reshape(64, 128)
-                power = second[:, 3 * CH - 128 : 3 * CH - 127].astype(jnp.float32)
-                scale = jnp.exp2(power) * (1.0 / 32767.0)
-                for half, word in enumerate((first, second)):
-                    real = (word >> 16).astype(jnp.float32) * scale
-                    imag = ((word << 16) >> 16).astype(jnp.float32) * scale
-                    both = jnp.concatenate([real, imag], axis=0)
-                    turned[pl.ds(half * 128, 128), :] = both.T
-                for b in range(3):
-                    hi, lo = split_bf16(turned[pl.ds(b * CH, 96), :])
-                    for j, item in enumerate((hi, lo, hi)):
-                        rows[par, pl.ds(i * 96, 96), pl.ds((b * 3 + j) * 128, 128)] = item
+            first, second = plane(a, par * 2), plane(a, par * 2 + 1)
+            scale0 = unit(second[:, 3 * CH - 128 : 3 * CH - 127])
+            scale1 = unit(second[:, 3 * CH - 127 : 3 * CH - 126])
+            scales.append(scale1)
+            for half, word in enumerate((first, second)):
+                scale = jnp.where(lax.rem(lane_left + half * 128, CH) < limit, scale0, scale1)
+                turned[par, pl.ds(half * 128, 128), :] = turned_rows(word, scale)
+        turned[2, pl.ds(0, 128), :] = turned_rows(plane(a, 4), jnp.where(lane_left < 63, scales[0], scales[1]))
+        for par in range(2):
+            for b in range(3):
+                blocks[par, b, pl.ds(0, CH), :] = turned[par, pl.ds(b * CH, CH), :]
+                blocks[par, b, pl.ds(CH, 21), :] = turned[2, pl.ds(63 * par + 21 * b, 21), :]
+                hi, lo = split_bf16(blocks[par, b])
+                for j, item in enumerate((hi, lo, hi)):
+                    rows[par, :, pl.ds((b * 3 + j) * 128, 128)] = item
             term = jnp.dot(
                 rows[par], basis[par, 3 * a : 3 * a + 3].reshape(1152, -1), preferred_element_type=jnp.float32
             )
@@ -314,33 +337,36 @@
             else:
                 total[par] += term
 
-    turned[pl.ds(256, turned.shape[0] - 256), :] = jnp.zeros((turned.shape[0] - 256, 128), jnp.float32)
+    blocks[...] = jnp.zeros(blocks.shape, jnp.float32)
     make_coded(0)
     send_coded(0)
     make_coded(1)
     send_coded(1)
-    forward_all(0)
-    forward_all(1)
+    for batch in range(2):
+        for a in range(2):
+            forward(a, batch)
+    for copy in own_m:
+        copy.wait()
     synthesize(0)
     synthesize(1)
 
     edge = HALF - 640
-    lanes = lax.broadcasted_iota(jnp.int32, (1, 128), 1)
-    for i in range(2):
-        even, odd = total[0, pl.ds(i * 96, CH), :], total[1, pl.ds(i * 96, CH), :]
-        plus = even + odd
-        minus = pltpu.roll(even - odd, edge, 1)
-        at = pl.ds(i * CH, CH)
-        out[at, :640] = plus[:, :640]
-        out[at, 640:768] = jnp.where(lanes < edge, plus[:, 640:], minus[:, :128])
-        out[at, 768:1408] = minus[:, 128:]
-        out[at, 1408:] = minus[:, : LON - 1408]
-
+    even, odd = total[0], total[1]
+    plus = even + odd
+    minus = pltpu.roll(even - odd, edge, 1)
+    count = out.shape[0]
+    out[:, :640] = plus[:count, :640]
+    out[:, 640:768] = jnp.where(lane_left < edge, plus[:, 640:], minus[:, :128])[:count]
+    out[:, 768:1408] = minus[:count, 128:]
+    out[:, 1408:] = minus[:count, : LON - 1408]
+
+    seven = pl.ds(0, 7)
     for a in range(2):
-        for copy in c_copies[a] + l_copies[a] + b_copies[a] + m_copies[a]:
-            copy.wait_send()
-    for copy in live.values():
-        copy.wait_send()
+        wait_bytes(packs_in.at[a, seven], c_send.at[a])
+        wait_bytes(table_in.at[a, seven], l_send.at[a])
+        wait_bytes(coef_all.at[a, seven], r_send.at[a])
+        wait_bytes(back.at[a, seven], b_send.at[a])
+        wait_bytes(words.at[a, seven], m_send.at[a])
 
 
 def synth_call(waves, table, packs):
@@ -351,7 +377,7 @@
     f32, bf16, s32 = jnp.float32, jnp.bfloat16, jnp.int32
     return pl.pallas_call(
         synth_kernel,
-        out_shape=jax.ShapeDtypeStruct((2 * CH, LON), f32),
+        out_shape=jax.ShapeDtypeStruct((105, LON), f32),
         in_specs=[vmem, vmem, vmem],
         out_specs=vmem,
         scratch_shapes=[
@@ -360,18 +386,20 @@
             pltpu.VMEM(packs.shape, f32),
             pltpu.VMEM((2, deg, 512), f32),
             pltpu.VMEM((2, RING, deg, 512), bf16),
-            pltpu.VMEM((2, RING, 10, 4, 128), s32),
-            pltpu.VMEM((2, RING, 10, 4, 128), s32),
-            pltpu.VMEM((2, RING, RING, 2, 4, 128), s32),
+            pltpu.VMEM((2, RING, 10, 256), s32),
+            pltpu.VMEM((2, RING, 5 * RING, 1, 128), s32),
+            pltpu.VMEM((2, RING, 5 * RING, 1, 128), s32),
+            pltpu.VMEM((2, RING, RING, 5, 1, 128), s32),
             pltpu.VMEM((deg_all, deg_all), bf16),
             pltpu.VMEM((6 * 64, 128), f32),
             pltpu.VMEM((2, 6, 384, 768), bf16),
-            pltpu.VMEM((272, 128), f32),
-            pltpu.VMEM((2, 192, 1152), bf16),
-            pltpu.VMEM((2, 192, 768), f32),
-            dma((2, 7)), dma((2, 7)), dma((2, 7)), dma((2, 7)),
-            dma((2, 2, 4, 2)), dma((2, 2, 4, 2)),
-            dma((2, 7)), dma((2, 7)), dma((2, 8, 7)), dma((2, 8, 7)), dma((20,)),
+            pltpu.VMEM((3, 256, 128), f32),
+            pltpu.VMEM((2, 3, 112, 128), f32),
+            pltpu.VMEM((2, 112, 1152), bf16),
+            pltpu.VMEM((2, 112, 768), f32),
+            dma((2,)), dma((2,)), dma((2,)), dma((2,)),
+            dma((2,)), dma((2, 2, 4, 2)),
+            dma((2,)), dma((2, 2)), dma((2,)), dma((2,)), dma((5, 2)),
         ],
         compiler_params=pltpu.CompilerParams(
             collective_id=0, has_side_effects=True, vmem_limit_bytes=48 << 20
@@ -381,11 +409,8 @@
 
 
 def body(pair_wave, legendre, coefs):
-    ma_i = lax.axis_index("ma")
     table, packs = pack_table(legendre), pack_coefs(coefs)
-    both = synth_call(pair_wave.reshape(1, -1), table, packs)
-    start = 105 * ma_i - CH * ((5 * ma_i) // 4)
-    return lax.dynamic_slice_in_dim(both, start, 105, axis=0)
+    return synth_call(pair_wave.reshape(1, -1), table, packs)
 
 
 def solution(mesh):

time: 63.1 us -> 56.9 us (0.902)
  Pallas kernels: 58.2 us -> 51.4 us
    pallas_call x1, Pallas kernels: 58.2 us -> 51.4 us  [synth_call(): pl.pallas_call(synth_kernel, out_shape=jax.ShapeDtypeStruct((105, LON), f...]
    unnamed x4 -> x7, local copies, waits for them, and re-layouts: 0.88 us -> 3 us
    slice x2, local copies, waits for them, and re-layouts: 0.22 us -> 1.28 us  [pack_table(): head = table[:, :8].reshape(2, RING, 24, row_count)]
    dynamic_slice x1 -> x0, local copies, waits for them, and re-layouts: 0.93 us -> none  [body(): return lax.dynamic_slice_in_dim(both, start, 105, axis=0)]
    slice x2, local copies, waits for them, and re-layouts: 1.04 us -> 0.13 us  [pack_table(): tail = table[:, 8:].reshape(2, RING, 6, row_count)]
    reshape x1, local copies, waits for them, and re-layouts: 0.75 us -> 0.01 us  [body(): return synth_call(pair_wave.reshape(1, -1), table, packs)]
where the time goes in v3:
time: 56.9 us; the launch traced here: 56.7 us
  Pallas kernels  51.4 us (90%)
  local copies, waits for them, and re-layouts  5.12 us (9%)
    pallas_call x1, Pallas kernels, synth_call(): pl.pallas_call(synth_kernel, out_shape=jax.ShapeDtypeStruct((105, LON), f...  51.4 us
    unnamed x7, local copies, waits for them, and re-layouts  3 us
    slice x2, local copies, waits for them, and re-layouts, pack_table(): head = table[:, :8].reshape(2, RING, 24, row_count)  1.28 us

profile of v3, /device:TPU:1, one launch (start us, length us, event | category | flops | bytes accessed | tf_op | source)
XLA Modules:
  0.0 56.7 jit_solution(7100428015881908882)
XLA Ops:
  0.0 1.1 %pad_slice_fusion.1 = bf16[48,8,768]{2,0,1:T(8,128)(2,1)S(1)} fusion(bf16[45,10,768]{2,0,1:T(8,128)(2,1)} %param.4), kind=kLoop, calls=%fused_computation.4 | loop fusion | bytes 1281024 | tf_op jit(solution)/shard_map/slice | solution.py:25
  1.1 0.0 copy-start
  1.1 0.2 copy.6
  1.3 0.9 %copy-done = bf16[45,10,768]{2,0,1:T(8,128)(2,1)S(1)} copy-done((bf16[45,10,768]{2,0,1:T(8,128)(2,1)S(1)}, bf16[45,10,768]{2,0,1:T(8,128)(2,1)}, u32[]{:S(2)}) %copy-start) | copy-done | bytes 691224
  2.2 0.1 copy.7
  2.4 0.1 reshape.23
  2.4 0.0 copy-start.1
  2.4 0.1 fusion.1.table
  2.5 0.9 %copy-done.1 = bf16[45,12,168]{2,0,1:T(8,128)(2,1)S(1)} copy-done((bf16[45,12,168]{2,0,1:T(8,128)(2,1)S(1)}, bf16[45,12,168]{2,0,1:T(8,128)(2,1)}, u32[]{:S(2)}) %copy-start.1) | copy-done | bytes 181464
  3.4 0.1 pad.18
  3.5 0.2 reshape.24
  3.6 0.1 copy.12
  3.8 0.0 copy-start.2
  3.8 0.2 reshape.25
  4.1 0.3 copy-done.2
  4.5 51.4 %synth.1 = f32[105,1440]{1,0:T(8,128)S(1)} custom-call(s32[1,360]{1,0:T(1,128)S(1)} %reshape.21.waves, bf16[2,8,32,768]{3,2,1,0:T(8,128)(2,1)S(1)} %fusion.1.table, bf16[2,8,48,128]{3,2,1,0:T(8,128)(2,1)S(1)} %copy.10.packs), custom_call_target="tpu_custom_call" | custom-call | tf_op jit(solution)/shard_map/synth/pallas_call | solution.py:378
  55.8 0.8 %copy.14 = f32[105,1440]{1,0:T(8,128)} copy(f32[105,1440]{1,0:T(8,128)S(1)} %synth.1) | data formatting | bytes 1209600
  (5 shorter events, 0.1 us)
Async XLA Ops:
  1.1 1.1 %copy-start = (bf16[45,10,768]{2,0,1:T(8,128)(2,1)S(1)}, bf16[45,10,768]{2,0,1:T(8,128)(2,1)}, u32[]{:S(2)}) copy-start(bf16[45,10,768]{2,0,1:T(8,128)(2,1)} %param.4) | copy-start | bytes 2073604
  2.4 1.0 %copy-start.1 = (bf16[45,12,168]{2,0,1:T(8,128)(2,1)S(1)}, bf16[45,12,168]{2,0,1:T(8,128)(2,1)}, u32[]{:S(2)}) copy-start(bf16[45,12,168]{2,0,1:T(8,128)(2,1)} %param.5) | copy-start | bytes 544324
  3.8 0.7 %copy-start.2 = (s32[360]{0:T(512)S(1)}, s32[360]{0:T(512)}, u32[]{:S(2)}) copy-start(s32[360]{0:T(512)} %param.3) | copy-start | bytes 4324

commit v4 on v3

--- a/solution.py
+++ b/solution.py
@@ -19,15 +19,6 @@
 MESH = pl.DeviceIdType.MESH
 
 
-def pack_table(legendre):
-    slots, rows_dev, row_count = legendre.shape
-    table = jnp.pad(legendre, ((0, 6 * RING - slots), (0, 0), (0, 0)))
-    head = table[:, :8].reshape(2, RING, 24, row_count)
-    tail = table[:, 8:].reshape(2, RING, 6, row_count)
-    tail = jnp.pad(tail, ((0, 0), (0, 0), (0, 2), (0, 0)))
-    return jnp.concatenate([head, tail], axis=2)
-
-
 def pack_coefs(coefs):
     slots, deg_dev, cols = coefs.shape
     x = jnp.pad(coefs, ((0, 6 * RING - slots), (0, 0), (0, 0)))
@@ -59,8 +50,8 @@
 
 
 def synth_kernel(
-    waves, table, packs, out,
-    table_in, packs_in, wide, coef_rows, coef_all, raw, coded, back, words,
+    waves, tables, packs, out,
+    table_raw, table_flat, pick, table, table_in, packs_in, wide, coef_rows, coef_all, raw, coded, back, words,
     perm, orders, basis, turned, blocks, rows, total,
     c_send, c_recv, l_send, l_recv, r_send, r_recv,
     b_send, b_recv, m_send, m_recv, own_sem,
@@ -82,6 +73,8 @@
         for a in range(2)
     ]
 
+    load = pltpu.make_async_copy(tables, table_raw, own_sem.at[5, 0])
+    load.start()
     barrier = pltpu.get_barrier_semaphore()
     targets = [peer(a, p) for a in range(2) for p in to[a]] + [(lat, p) for p in ma_to]
     for target in targets:
@@ -109,6 +102,25 @@
             p = to[a][k]
             remote(packs.at[a, p], packs_in.at[a, group[a]], c_send.at[a], c_recv.at[a], peer(a, p))
     own_c = [keep_local(packs.at[a, group[a]], packs_in.at[a, group[a]], own_sem.at[0, a]) for a in range(2)]
+
+    lats, slots, deg_all = tables.shape
+    stride = 48
+    table_flat[...] = jnp.zeros(table_flat.shape, table_flat.dtype)
+    row = lax.broadcasted_iota(jnp.int32, (RING * 32, 1), 0)
+    inner = lax.rem(row, 32)
+    member = jnp.where(inner < 24, inner // 8, (inner - 24) // 2)
+    at_lat = jnp.where(inner < 24, lax.rem(inner, 8), 8 + lax.rem(inner, 2))
+    for a in range(2):
+        want = at_lat * stride + a * 3 * RING + row // 32 * 3 + member
+        want = jnp.where(inner < 30, want, -1)
+        lanes = lax.broadcasted_iota(jnp.int32, (RING * 32, lats * stride), 1)
+        pick[a] = jnp.where(lanes == want, 1.0, 0.0).astype(jnp.bfloat16)
+    load.wait()
+    for i in range(lats):
+        table_flat[pl.ds(i * stride, slots), :] = table_raw[i]
+    for a in range(2):
+        moved = jnp.dot(pick[a], table_flat[...], preferred_element_type=jnp.float32)
+        table[a] = moved.astype(jnp.bfloat16).reshape(RING, 32, deg_all)
     own_l = [keep_local(table.at[a, group[a]], table_in.at[a, group[a]], own_sem.at[1, a]) for a in range(2)]
 
     def send_table(ks):
@@ -342,8 +354,8 @@
     send_coded(0)
     make_coded(1)
     send_coded(1)
-    for batch in range(2):
-        for a in range(2):
+    for a in range(2):
+        for batch in range(2):
             forward(a, batch)
     for copy in own_m:
         copy.wait()
@@ -369,19 +381,24 @@
         wait_bytes(words.at[a, seven], m_send.at[a])
 
 
-def synth_call(waves, table, packs):
+def synth_call(waves, tables, packs):
     vmem = pl.BlockSpec(memory_space=pltpu.VMEM)
     dma = pltpu.SemaphoreType.DMA
     deg = packs.shape[2] // 4 * RING
-    deg_all = table.shape[3]
+    lats, slots, deg_all = tables.shape
+    table = (2, RING, 32, deg_all)
     f32, bf16, s32 = jnp.float32, jnp.bfloat16, jnp.int32
     return pl.pallas_call(
         synth_kernel,
         out_shape=jax.ShapeDtypeStruct((105, LON), f32),
-        in_specs=[vmem, vmem, vmem],
+        in_specs=[vmem, pl.BlockSpec(memory_space=pltpu.HBM), vmem],
         out_specs=vmem,
         scratch_shapes=[
-            pltpu.VMEM(table.shape, bf16),
+            pltpu.VMEM(tables.shape, bf16),
+            pltpu.VMEM((lats * 48, deg_all), bf16),
+            pltpu.VMEM((2, RING * 32, lats * 48), bf16),
+            pltpu.VMEM(table, bf16),
+            pltpu.VMEM(table, bf16),
             pltpu.VMEM(packs.shape, bf16),
             pltpu.VMEM(packs.shape, f32),
             pltpu.VMEM((2, deg, 512), f32),
@@ -399,18 +416,19 @@
             pltpu.VMEM((2, 112, 768), f32),
             dma((2,)), dma((2,)), dma((2,)), dma((2,)),
             dma((2,)), dma((2, 2, 4, 2)),
-            dma((2,)), dma((2, 2)), dma((2,)), dma((2,)), dma((5, 2)),
+            dma((2,)), dma((2, 2)), dma((2,)), dma((2,)), dma((6, 2)),
         ],
         compiler_params=pltpu.CompilerParams(
             collective_id=0, has_side_effects=True, vmem_limit_bytes=48 << 20
         ),
         name="synth",
-    )(waves, table, packs)
+    )(waves, tables, packs)
 
 
 def body(pair_wave, legendre, coefs):
-    table, packs = pack_table(legendre), pack_coefs(coefs)
-    return synth_call(pair_wave.reshape(1, -1), table, packs)
+    return synth_call(
+        pair_wave.reshape(1, -1), jnp.transpose(legendre, (1, 0, 2)), pack_coefs(coefs)
+    )
 
 
 def solution(mesh):

time: 56.9 us -> 56.3 us (0.989)
  local copies, waits for them, and re-layouts: 5.12 us -> 4.13 us
    slice x4 -> x0, local copies, waits for them, and re-layouts: 1.41 us -> none  [the longest x2 1.28 us: pack_table(): head = table[:, :8].reshape(2, RING, 24, row_count)]
    unnamed x7 -> x3, local copies, waits for them, and re-layouts: 3 us -> 1.83 us
    pad x1, local copies, waits for them, and re-layouts: 0.05 us -> 1.01 us  [pack_coefs(): x = jnp.pad(coefs, ((0, 6 * RING - slots), (0, 0), (0, 0)))]
    reshape x2 -> x1, local copies, waits for them, and re-layouts: 0.07 us -> 0.68 us  [body(): pair_wave.reshape(1, -1)]
    pallas_call x1, Pallas kernels: 51.4 us -> 51.9 us  [synth_call(): pl.pallas_call(synth_kernel, out_shape=jax.ShapeDtypeStruct((105, LON), f...]
where the time goes in v4:
time: 56.3 us; the launch traced here: 56.1 us
  Pallas kernels  51.9 us (92%)
  local copies, waits for them, and re-layouts  4.13 us (7%)
    pallas_call x1, Pallas kernels, synth_call(): pl.pallas_call(synth_kernel, out_shape=jax.ShapeDtypeStruct((105, LON), f...  51.9 us
    unnamed x3, local copies, waits for them, and re-layouts  1.83 us

profile of v4, /device:TPU:1, one launch (start us, length us, event | category | flops | bytes accessed | tf_op | source)
XLA Modules:
  0.0 56.1 jit_solution(6705511818288413723)
XLA Ops:
  0.0 0.7 %reshape.15.waves = s32[1,360]{1,0:T(1,128)S(1)} reshape(s32[360]{0:T(512)} %param.3) | data formatting | bytes 2880 | tf_op jit(solution)/shard_map/reshape | solution.py:430
  0.7 1.0 %pad.8 = bf16[48,12,168]{2,0,1:T(8,128)(2,1)S(1)} pad(bf16[45,12,168]{2,0,1:T(8,128)(2,1)} %param.5, bf16[]{:T(256)} %constant.2.clone.1), padding=0_3x0_0x0_0 | pad | bytes 374978 | tf_op jit(solution)/shard_map/jit(_pad)/pad | solution.py:24
  1.7 0.2 reshape.16
  1.9 0.1 copy.8
  2.0 0.2 reshape.17
  2.2 0.0 copy-start
  2.4 1.0 %copy-done = bf16[45,10,768]{2,0,1:T(8,128)(2,1)S(1)} copy-done((bf16[45,10,768]{2,0,1:T(8,128)(2,1)S(1)}, bf16[45,10,768]{2,0,1:T(8,128)(2,1)}, u32[]{:S(2)}) %copy-start) | copy-done | bytes 691224
  3.3 51.9 %synth.1 = f32[105,1440]{1,0:T(8,128)S(1)} custom-call(s32[1,360]{1,0:T(1,128)S(1)} %reshape.15.waves, bf16[10,45,768]{2,1,0:T(8,128)(2,1)S(1)} %bitcast.13, bf16[2,8,48,128]{3,2,1,0:T(8,128)(2,1)S(1)} %copy.6.packs), custom_call_target="tpu_custom_call" | custom-call | tf_op jit(solution)/shard_map/synth/pallas_call | solution.py:391
  55.3 0.8 %copy.10 = f32[105,1440]{1,0:T(8,128)} copy(f32[105,1440]{1,0:T(8,128)S(1)} %synth.1) | data formatting | bytes 1209600
  (3 shorter events, 0.1 us)
Async XLA Ops:
  2.2 1.1 %copy-start = (bf16[45,10,768]{2,0,1:T(8,128)(2,1)S(1)}, bf16[45,10,768]{2,0,1:T(8,128)(2,1)}, u32[]{:S(2)}) copy-start(bf16[45,10,768]{2,0,1:T(8,128)(2,1)} %param.4) | copy-start | bytes 2073604

commit v5 on v4

--- a/solution.py
+++ b/solution.py
@@ -19,16 +19,6 @@
 MESH = pl.DeviceIdType.MESH
 
 
-def pack_coefs(coefs):
-    slots, deg_dev, cols = coefs.shape
-    x = jnp.pad(coefs, ((0, 6 * RING - slots), (0, 0), (0, 0)))
-    x = x.reshape(2, RING, 3, deg_dev, 2, CH).transpose(0, 1, 4, 3, 2, 5)
-    x = x.reshape(2, RING, 2, deg_dev, 3 * CH)
-    x = jnp.pad(x, ((0, 0),) * 4 + ((0, 256 - 3 * CH),))
-    x = x.reshape(2, RING, 2, deg_dev, 2, 128).transpose(0, 1, 2, 4, 3, 5)
-    return x.reshape(2, RING, 4 * deg_dev, 128)
-
-
 def poly(coefficients, square):
     value = jnp.float32(coefficients[-1])
     for coefficient in coefficients[-2::-1]:
@@ -50,8 +40,8 @@
 
 
 def synth_kernel(
-    waves, tables, packs, out,
-    table_raw, table_flat, pick, table, table_in, packs_in, wide, coef_rows, coef_all, raw, coded, back, words,
+    waves_in, tables, coefs, out,
+    waves, coef_raw, coef_flat, coef_pick, packs, table_raw, table_flat, pick, table, table_in, packs_in, wide, coef_rows, coef_all, raw, coded, back, words,
     perm, orders, basis, turned, blocks, rows, total,
     c_send, c_recv, l_send, l_recv, r_send, r_recv,
     b_send, b_recv, m_send, m_recv, own_sem,
@@ -73,12 +63,46 @@
         for a in range(2)
     ]
 
+    load_c = pltpu.make_async_copy(coefs, coef_raw, own_sem.at[5, 1])
+    load_c.start()
     load = pltpu.make_async_copy(tables, table_raw, own_sem.at[5, 0])
     load.start()
+    load_w = pltpu.make_async_copy(waves_in, waves, own_sem.at[6, 0])
+    load_w.start()
     barrier = pltpu.get_barrier_semaphore()
     targets = [peer(a, p) for a in range(2) for p in to[a]] + [(lat, p) for p in ma_to]
     for target in targets:
         pl.semaphore_signal(barrier, inc=1, device_id=target, device_id_type=MESH)
+
+    lats, slots, deg_all = tables.shape
+    deg_dev, _, cols = coefs.shape
+    stride = 48
+    coef_flat[...] = jnp.zeros(coef_flat.shape, coef_flat.dtype)
+    row = lax.broadcasted_iota(jnp.int32, (16 * 2 * RING, 1), 0)
+    inner = lax.rem(row, 16)
+    lanes = lax.broadcasted_iota(jnp.int32, (16 * 2 * RING, deg_dev * stride), 1)
+    for b in range(3):
+        want = jnp.where(inner < deg_dev, inner * stride + row // 16 * 3 + b, -1)
+        coef_pick[b] = jnp.where(lanes == want, 1.0, 0.0).astype(jnp.bfloat16)
+    load_c.wait()
+    for i in range(deg_dev):
+        coef_flat[pl.ds(i * stride, slots), :cols] = coef_raw[i]
+    real, imag = None, None
+    lane_c = lax.broadcasted_iota(jnp.int32, (1, 256), 1)
+    for b in range(3):
+        moved = jnp.dot(coef_pick[b], coef_flat[...], preferred_element_type=jnp.float32)
+        first = pltpu.roll(moved, b * CH, 1) if b else moved
+        second = pltpu.roll(moved, (b * CH - CH) % 256, 1) if b != 1 else moved
+        here = (lane_c >= b * CH) & (lane_c < b * CH + CH)
+        real = jnp.where(here, first, 0.0 if real is None else real)
+        imag = jnp.where(here, second, 0.0 if imag is None else imag)
+    for a in range(2):
+        for g in range(RING):
+            at = (a * RING + g) * 16
+            for t in range(4):
+                piece = (real if t < 2 else imag)[at : at + deg_dev, t % 2 * 128 : t % 2 * 128 + 128]
+                wide[a, g, pl.ds(t * deg_dev, deg_dev), :] = piece
+        packs[a] = wide[a].astype(jnp.bfloat16)
     pl.semaphore_wait(barrier, len(targets))
 
     def remote(src, dst, send, recv, target):
@@ -103,8 +127,6 @@
             remote(packs.at[a, p], packs_in.at[a, group[a]], c_send.at[a], c_recv.at[a], peer(a, p))
     own_c = [keep_local(packs.at[a, group[a]], packs_in.at[a, group[a]], own_sem.at[0, a]) for a in range(2)]
 
-    lats, slots, deg_all = tables.shape
-    stride = 48
     table_flat[...] = jnp.zeros(table_flat.shape, table_flat.dtype)
     row = lax.broadcasted_iota(jnp.int32, (RING * 32, 1), 0)
     inner = lax.rem(row, 32)
@@ -131,9 +153,10 @@
 
     send_table(TABLE_STEPS[0])
 
-    pairs = waves.shape[1]
+    pairs = waves.shape[0]
     per = pairs // RING
-    wave_row = waves[...].astype(jnp.float32)
+    load_w.wait()
+    wave_row = waves[...].reshape(1, pairs).astype(jnp.float32)
 
     def waves_of(slot):
         lanes = lax.broadcasted_iota(jnp.int32, (slot.shape[0], pairs), 1)
@@ -172,7 +195,6 @@
         lax.fori_loop(start, start + count, lambda n, c: (make_basis(n), c)[1], 0)
 
     column = lax.broadcasted_iota(jnp.int32, (1, table.shape[3]), 1)
-    deg_dev = packs.shape[2] // 4
     deg = RING * deg_dev
     turned_column = (
         lax.rem(column, deg) // deg_dev * deg + column // deg * deg_dev + lax.rem(column, deg_dev)
@@ -381,26 +403,32 @@
         wait_bytes(words.at[a, seven], m_send.at[a])
 
 
-def synth_call(waves, tables, packs):
+def synth_call(waves, tables, coefs):
     vmem = pl.BlockSpec(memory_space=pltpu.VMEM)
     dma = pltpu.SemaphoreType.DMA
-    deg = packs.shape[2] // 4 * RING
+    packs = (2, RING, 4 * coefs.shape[0], 128)
+    deg = coefs.shape[0] * RING
     lats, slots, deg_all = tables.shape
     table = (2, RING, 32, deg_all)
     f32, bf16, s32 = jnp.float32, jnp.bfloat16, jnp.int32
     return pl.pallas_call(
         synth_kernel,
         out_shape=jax.ShapeDtypeStruct((105, LON), f32),
-        in_specs=[vmem, pl.BlockSpec(memory_space=pltpu.HBM), vmem],
+        in_specs=[pl.BlockSpec(memory_space=pltpu.HBM)] * 3,
         out_specs=vmem,
         scratch_shapes=[
+            pltpu.VMEM(waves.shape, s32),
+            pltpu.VMEM(coefs.shape, bf16),
+            pltpu.VMEM((coefs.shape[0] * 48, 256), bf16),
+            pltpu.VMEM((3, 16 * 2 * RING, coefs.shape[0] * 48), bf16),
+            pltpu.VMEM(packs, bf16),
             pltpu.VMEM(tables.shape, bf16),
             pltpu.VMEM((lats * 48, deg_all), bf16),
             pltpu.VMEM((2, RING * 32, lats * 48), bf16),
             pltpu.VMEM(table, bf16),
             pltpu.VMEM(table, bf16),
-            pltpu.VMEM(packs.shape, bf16),
-            pltpu.VMEM(packs.shape, f32),
+            pltpu.VMEM(packs, bf16),
+            pltpu.VMEM(packs, f32),
             pltpu.VMEM((2, deg, 512), f32),
             pltpu.VMEM((2, RING, deg, 512), bf16),
             pltpu.VMEM((2, RING, 10, 256), s32),
@@ -416,19 +444,19 @@
             pltpu.VMEM((2, 112, 768), f32),
             dma((2,)), dma((2,)), dma((2,)), dma((2,)),
             dma((2,)), dma((2, 2, 4, 2)),
-            dma((2,)), dma((2, 2)), dma((2,)), dma((2,)), dma((6, 2)),
+            dma((2,)), dma((2, 2)), dma((2,)), dma((2,)), dma((7, 2)),
         ],
         compiler_params=pltpu.CompilerParams(
             collective_id=0, has_side_effects=True, vmem_limit_bytes=48 << 20
         ),
         name="synth",
-    )(waves, tables, packs)
+    )(waves, tables, coefs)
 
 
 def body(pair_wave, legendre, coefs):
-    return synth_call(
-        pair_wave.reshape(1, -1), jnp.transpose(legendre, (1, 0, 2)), pack_coefs(coefs)
-    )
+    tables, coefs = jnp.transpose(legendre, (1, 0, 2)), jnp.transpose(coefs, (1, 0, 2))
+    args = (pair_wave, tables, coefs)
+    return synth_call(*(pltpu.with_memory_space_constraint(x, pltpu.HBM) for x in args))
 
 
 def solution(mesh):

time: 56.3 us -> 52.4 us (0.931)
  local copies, waits for them, and re-layouts: 4.13 us -> 0.85 us
    reshape x5 -> x0, local copies, waits for them, and re-layouts: 1.21 us -> none  [the longest x1 0.68 us: body(): pair_wave.reshape(1, -1)]
    pad x1 -> x0, local copies, waits for them, and re-layouts: 1.01 us -> none  [pack_coefs(): x = jnp.pad(coefs, ((0, 6 * RING - slots), (0, 0), (0, 0)))]
    unnamed x3 -> x1, local copies, waits for them, and re-layouts: 1.83 us -> 0.85 us
    pallas_call x1, Pallas kernels: 51.9 us -> 51.4 us  [synth_call(): pl.pallas_call(synth_kernel, out_shape=jax.ShapeDtypeStruct((105, LON), f...]
where the time goes in v5:
time: 52.4 us; the launch traced here: 52.2 us
  Pallas kernels  51.4 us (98%)
  local copies, waits for them, and re-layouts  0.85 us (2%)
    pallas_call x1, Pallas kernels, synth_call(): pl.pallas_call(synth_kernel, out_shape=jax.ShapeDtypeStruct((105, LON), f...  51.4 us

profile of v5, /device:TPU:1, one launch (start us, length us, event | category | flops | bytes accessed | tf_op | source)
XLA Modules:
  0.0 52.2 jit_solution(11726339193806683433)
XLA Ops:
  0.0 51.4 %synth.1 = f32[105,1440]{1,0:T(8,128)S(1)} custom-call(s32[360]{0:T(512)} %waves_in.1, bf16[10,45,768]{2,1,0:T(8,128)(2,1)} %bitcast.2, bf16[12,45,168]{2,1,0:T(8,128)(2,1)} %bitcast.3), custom_call_target="tpu_custom_call" | custom-call | tf_op jit(solution)/shard_map/synth/pallas_call | solution.py:414
  51.4 0.8 %copy.5 = f32[105,1440]{1,0:T(8,128)} copy(f32[105,1440]{1,0:T(8,128)S(1)} %synth.1) | data formatting | bytes 1209600

commit v6 on v5

--- a/solution.py
+++ b/solution.py
@@ -42,7 +42,7 @@
 def synth_kernel(
     waves_in, tables, coefs, out,
     waves, coef_raw, coef_flat, coef_pick, packs, table_raw, table_flat, pick, table, table_in, packs_in, wide, coef_rows, coef_all, raw, coded, back, words,
-    perm, orders, basis, turned, blocks, rows, total,
+    masked, perm, orders, basis, turned, blocks, rows, total,
     c_send, c_recv, l_send, l_recv, r_send, r_recv,
     b_send, b_recv, m_send, m_recv, own_sem,
 ):
@@ -214,34 +214,38 @@
         return 4 if s == dirn else 3
 
     live = {}
-    for a in range(2):
-        own_c[a].wait()
-        wait_bytes(packs_in.at[a, pl.ds(0, 7)], c_recv.at[a])
-        wide[a] = packs_in[a].astype(jnp.float32)
-        for s in range(RING):
-            for t in range(4):
-                piece = wide[a, s, pl.ds(t * deg_dev, deg_dev), :]
-                coef_rows[a, pl.ds(s * deg_dev, deg_dev), pl.ds(t * 128, 128)] = piece
-        coef_all[a, place[a]] = coef_rows[a].astype(jnp.bfloat16)
-        for s in range(2):
+    half_rows, half_ring = deg // 2, RING // 2
+    for s in range(2):
+        for a in range(2):
+            if s == 0:
+                own_c[a].wait()
+                wait_bytes(packs_in.at[a, pl.ds(0, 7)], c_recv.at[a])
+            part = pl.ds(s * half_ring, half_ring)
+            wide[a, part] = packs_in[a, part].astype(jnp.float32)
+            for n in range(s * half_ring, (s + 1) * half_ring):
+                for t in range(4):
+                    piece = wide[a, n, pl.ds(t * deg_dev, deg_dev), :]
+                    coef_rows[a, pl.ds(n * deg_dev, deg_dev), pl.ds(t * 128, 128)] = piece
+            part = pl.ds(s * half_rows, half_rows)
+            coef_all[a, place[a], part] = coef_rows[a, part].astype(jnp.bfloat16)
             for dirn in range(2):
                 live[a, dirn, 0, s] = ring_send(a, dirn, 0, s)
 
-    def ring_step(a, step):
-        for s in range(2):
-            for dirn in range(2):
-                if step <= hops(dirn, s):
-                    live[a, dirn, step - 1, s].wait_recv()
-                    if step < hops(dirn, s):
-                        live[a, dirn, step, s] = ring_send(a, dirn, step, s)
+    def ring_step(a, step, s):
+        for dirn in range(2):
+            if step <= hops(dirn, s):
+                live[a, dirn, step - 1, s].wait_recv()
+                if step < hops(dirn, s):
+                    live[a, dirn, step, s] = ring_send(a, dirn, step, s)
 
     for step in range(1, 4):
         send_table(TABLE_STEPS[step])
         if BASIS_STEPS[step]:
             make_bases(made, BASIS_STEPS[step])
             made += BASIS_STEPS[step]
-        for a in range(2):
-            ring_step(a, step)
+        for s in range(2):
+            for a in range(2):
+                ring_step(a, step, s)
 
     row = lax.broadcasted_iota(jnp.int32, (32, 1), 0)
     member = jnp.minimum(jnp.where(row < 24, row // 8, (row - 24) // 2), 2)
@@ -249,8 +253,7 @@
     lane_out = lax.broadcasted_iota(jnp.int32, (1, 256), 1)
     lane_left = lax.broadcasted_iota(jnp.int32, (1, 128), 1)
 
-    def make_coded(a):
-        ring_step(a, 4)
+    def mask_table(a):
         own_l[a].wait()
         wait_bytes(table_in.at[a, pl.ds(0, 7)], l_recv.at[a])
         u = waves_of(ma * per + jnp.minimum(a * 3 * RING + group[a] * 3 + member, per - 1))
@@ -268,12 +271,17 @@
             rows_a = jnp.dot(flat, perm[...], preferred_element_type=jnp.float32).reshape(RING, 32, -1)
             at = turned_column
         at = at.astype(jnp.float32)
-        rhs = coef_all[a].reshape(-1, 512)
         for par in range(2):
             low, high = bounds[par]
             keep = ((at >= low) & (at < high))[None]
-            lhs = jnp.where(keep, rows_a, 0.0).astype(jnp.bfloat16).reshape(RING * 32, -1)
-            sums = jnp.dot(lhs, rhs, preferred_element_type=jnp.float32)
+            masked[a, par] = jnp.where(keep, rows_a, 0.0).astype(jnp.bfloat16).reshape(RING * 32, -1)
+
+    def make_coded(a):
+        ring_step(a, 4, 0)
+        ring_step(a, 4, 1)
+        rhs = coef_all[a].reshape(-1, 512)
+        for par in range(2):
+            sums = jnp.dot(masked[a, par], rhs, preferred_element_type=jnp.float32)
             sums = sums.reshape(RING, 4, 8, 512)
             tail = sums[:, 3]
             two, four = pltpu.roll(tail, 6, 1), pltpu.roll(tail, 4, 1)
@@ -372,6 +380,8 @@
                 total[par] += term
 
     blocks[...] = jnp.zeros(blocks.shape, jnp.float32)
+    mask_table(0)
+    mask_table(1)
     make_coded(0)
     send_coded(0)
     make_coded(1)
@@ -435,6 +445,7 @@
             pltpu.VMEM((2, RING, 5 * RING, 1, 128), s32),
             pltpu.VMEM((2, RING, 5 * RING, 1, 128), s32),
             pltpu.VMEM((2, RING, RING, 5, 1, 128), s32),
+            pltpu.VMEM((2, 2, RING * 32, deg_all), bf16),
             pltpu.VMEM((deg_all, deg_all), bf16),
             pltpu.VMEM((6 * 64, 128), f32),
             pltpu.VMEM((2, 6, 384, 768), bf16),

time: 52.4 us -> 51.7 us (0.987)
  Pallas kernels: 51.4 us -> 50.7 us
    pallas_call x1, Pallas kernels: 51.4 us -> 50.7 us  [synth_call(): pl.pallas_call(synth_kernel, out_shape=jax.ShapeDtypeStruct((105, LON), f...]
where the time goes in v6:
time: 51.7 us; the launch traced here: 51.5 us
  Pallas kernels  50.7 us (98%)
  local copies, waits for them, and re-layouts  0.85 us (2%)
    pallas_call x1, Pallas kernels, synth_call(): pl.pallas_call(synth_kernel, out_shape=jax.ShapeDtypeStruct((105, LON), f...  50.7 us

profile of v6, /device:TPU:1, one launch (start us, length us, event | category | flops | bytes accessed | tf_op | source)
XLA Modules:
  0.0 51.5 jit_solution(424061842287225979)
XLA Ops:
  0.0 50.7 %synth.1 = f32[105,1440]{1,0:T(8,128)S(1)} custom-call(s32[360]{0:T(512)} %waves_in.1, bf16[10,45,768]{2,1,0:T(8,128)(2,1)} %bitcast.2, bf16[12,45,168]{2,1,0:T(8,128)(2,1)} %bitcast.3), custom_call_target="tpu_custom_call" | custom-call | tf_op jit(solution)/shard_map/synth/pallas_call | solution.py:424
  50.7 0.8 %copy.5 = f32[105,1440]{1,0:T(8,128)} copy(f32[105,1440]{1,0:T(8,128)S(1)} %synth.1) | data formatting | bytes 1209600
